TPU v7x, 32 devices: a whole 2x2x4 slice. The times are simulated.
32 devices in a mesh: row: 4 (over x, core), col: 8 (over z, y).
Axes of the slice: x: 2, y: 2, z: 4, core: 2. Of those that a mesh axis runs over, the one named last changes fastest.
Arguments:
- x_vals: bfloat16 [256, 32, 4096], P(('row', 'col')), may hold values from -6 to 6
- occupancy: int32 [256, 32], P(('row', 'col')), may hold values from 0 to 1, as said below
- perm: int32 [256], replicated, may hold values from 0 to 255, as said below
Outputs:
- sign_iterate_next: bfloat16 [16384, 16384], P('row', 'col')
Inputs may be any that keep to these rules, and one draw needn't show every extreme that they name: occupancy[i, s] = 1 marks block (i, (i - 16 + s) mod 256) as present; the diagonal slot s = 16 is always 1, and some row has all 32 slots 1. perm is a permutation with perm[j] = a(j mod (8)) * 32 + b(j div (8)) for permutations a and b; so the 32 band columns of any row fall exactly 4 times into each aligned run of 32 new indices, and each aligned run of 64 initial indices has exactly 16 members in each aligned run of 64 new indices.
All inputs are finite; a program needn't handle non-finite values.
Results may differ from a plain program's by a relative error of at most 0.0017.
Values may be sent and summed in bfloat16 or wider, within the bound.
A program may use at most 128 MiB of HBM per device.

v0:
```python
import jax
import jax.numpy as jnp
from jax import lax
from jax.experimental import pallas as pl
from jax.experimental.pallas import tpu as pltpu
from jax.sharding import PartitionSpec as P

BLOCK_EDGE = 64


def multiply_kernel(order_ref, left_ref, far0, far1, far2, far3, out_ref):
    width = out_ref.shape[-1]
    left = left_ref[...].reshape(-1, width)
    right = jnp.concatenate([r[...].reshape(-1, width) for r in (far0, far1, far2, far3)], axis=0)
    update = jnp.dot(left, right, preferred_element_type=jnp.float32).reshape(out_ref.shape)

    @pl.when(pl.program_id(1) == 0)
    def _():
        out_ref[...] = update

    @pl.when(pl.program_id(1) != 0)
    def _():
        out_ref[...] += update


def banded_product(left, far, order, residue_major, slots):
    panels, halves, count, edge, width = left.shape
    chunk = slots // 2
    chunks = count // chunk

    def far_spec(position):
        def chunk_of(g):
            return lax.rem(2 * g + chunks - 1 + lax.rem(position + 1 + 2 * g, 4), chunks)

        if residue_major:
            return pl.BlockSpec(
                (1, chunk, edge, width), lambda g, p, order: (order[p], chunk_of(g), 0, 0)
            )
        return pl.BlockSpec(
            (chunk, 1, edge, width), lambda g, p, order: (chunk_of(g), order[p], 0, 0)
        )

    return pl.pallas_call(
        multiply_kernel,
        out_shape=jax.ShapeDtypeStruct((halves, count, edge, width), jnp.float32),
        grid_spec=pltpu.PrefetchScalarGridSpec(
            num_scalar_prefetch=1,
            grid=(count // slots, panels),
            in_specs=[
                pl.BlockSpec(
                    (1, halves, slots, edge, width), lambda g, p, order: (p, 0, g, 0, 0)
                )
            ]
            + [far_spec(position) for position in range(4)],
            out_specs=pl.BlockSpec((halves, slots, edge, width), lambda g, p, order: (0, g, 0, 0)),
        ),
        compiler_params=pltpu.CompilerParams(dimension_semantics=("arbitrary", "arbitrary")),
    )(order, left, far, far, far, far)


def spread_kernel(source_ref, target_ref, rows_ref, out_ref):
    slots = rows_ref.shape[-1] // BLOCK_EDGE
    q, n = pl.program_id(0), pl.program_id(1)
    row = q * pl.num_programs(1) + source_ref[n]
    out_ref[...] = jnp.zeros_like(out_ref)
    for v in range(slots):
        block = rows_ref[0, 0, :, v * BLOCK_EDGE : (v + 1) * BLOCK_EDGE].astype(jnp.float32)
        target = target_ref[row * slots + v]
        odd = lax.rem(target, 2)
        pair = jnp.concatenate(
            [block * (1 - odd).astype(jnp.float32), block * odd.astype(jnp.float32)], axis=1
        ).astype(out_ref.dtype)
        at = pl.multiple_of((target // 2) * (2 * BLOCK_EDGE), 2 * BLOCK_EDGE)
        out_ref[:, pl.ds(at, 2 * BLOCK_EDGE)] += pair


def spread(rows, source, target, panel_cols):
    halves, count, edge, width = rows.shape
    return pl.pallas_call(
        spread_kernel,
        out_shape=jax.ShapeDtypeStruct((halves * count * edge, panel_cols * edge), rows.dtype),
        grid_spec=pltpu.PrefetchScalarGridSpec(
            num_scalar_prefetch=2,
            grid=(halves, count),
            in_specs=[
                pl.BlockSpec((1, 1, edge, width), lambda q, n, source, target: (q, source[n], 0, 0))
            ],
            out_specs=pl.BlockSpec(
                (edge, panel_cols * edge), lambda q, n, source, target: (q * count + n, 0)
            ),
        ),
        compiler_params=pltpu.CompilerParams(dimension_semantics=("arbitrary", "arbitrary")),
    )(source, target, rows)


def band_index(m, row_residue, col_residue, slots):
    first = m - slots // 2 + (col_residue < row_residue).astype(jnp.int32)
    v = jnp.arange(slots, dtype=jnp.int32)
    first = first[..., None]
    return first + (v - first) % slots


def widen(values, index, slots):
    high = (index % (2 * slots)) >= slots
    high = jnp.repeat(high, BLOCK_EDGE, axis=-1)[..., None, :]
    zero = jnp.zeros((), values.dtype)
    return jnp.concatenate(
        [jnp.where(high, zero, values), jnp.where(high, values, zero)], axis=-1
    )


def shards(x_vals, occupancy, perm):
    row_devices = lax.axis_size("row")
    panels = lax.axis_size("col")
    own_row = lax.axis_index("row")
    own_col = lax.axis_index("col")
    local_rows, band_extent, block_area = x_vals.shape
    block_count = perm.shape[0]
    panel_cols = block_count // panels
    halves = panels // row_devices
    slots = band_extent // panels
    lanes = slots * BLOCK_EDGE

    panel_of_residue = perm[:panels] // panel_cols
    residue_ids = jnp.arange(panels, dtype=jnp.int32)
    order = jnp.sum(
        jnp.where(panel_of_residue[None, :] == residue_ids[:, None], residue_ids[None, :], 0), axis=1
    ).astype(jnp.int32)
    inside = perm[::panels] % panel_cols
    m_ids = jnp.arange(panel_cols, dtype=jnp.int32)
    source = jnp.sum(
        jnp.where(inside[None, :] == m_ids[:, None], m_ids[None, :], 0), axis=1
    ).astype(jnp.int32)
    own_residue = order[own_col]
    row_residues = lax.dynamic_slice_in_dim(order, own_row * halves, halves)

    first_row = (own_row * panels + own_col) * local_rows
    row_ids = first_row + jnp.arange(local_rows, dtype=jnp.int32)
    cols = (
        row_ids[:, None] - band_extent // 2 + jnp.arange(band_extent, dtype=jnp.int32)[None, :]
    ) % block_count
    placed = (
        (occupancy[:, :, None, None] == 1)
        & ((cols % panels)[:, :, None, None] == order[None, None, :, None])
        & (
            ((cols // panels) % slots)[:, :, None, None]
            == jnp.arange(slots, dtype=jnp.int32)[None, None, None, :]
        )
    ).astype(jnp.bfloat16)
    kept = jnp.sum(placed.astype(jnp.float32), axis=1).astype(jnp.bfloat16)
    every_kept = lax.all_gather(
        kept.reshape(local_rows, panels * slots), ("row", "col"), axis=0, tiled=True
    ).reshape(panel_cols, panels, panels, slots)
    values = jnp.einsum(
        "kspt,ksf->pktf", placed, x_vals, preferred_element_type=jnp.float32
    ).astype(jnp.bfloat16)
    values = (
        values.reshape(panels, local_rows, slots, BLOCK_EDGE, BLOCK_EDGE)
        .transpose(0, 1, 3, 2, 4)
        .reshape(panels, local_rows, BLOCK_EDGE, lanes)
    )
    first = lax.all_to_all(values, "col", split_axis=0, concat_axis=0, tiled=True)
    first = first.reshape(panels * local_rows, BLOCK_EDGE, lanes)
    far = lax.all_gather(first, "row", axis=0, tiled=True).reshape(
        panel_cols, panels, BLOCK_EDGE, lanes
    )
    tile = jnp.stack(
        [
            lax.dynamic_index_in_dim(far, row_residues[q], axis=1, keepdims=False)
            for q in range(halves)
        ]
    )
    own_kept = lax.dynamic_index_in_dim(every_kept, own_col, axis=2, keepdims=False)
    wanted = jnp.stack(
        [
            lax.dynamic_index_in_dim(own_kept, row_residues[q], axis=1, keepdims=False)
            for q in range(halves)
        ]
    )
    wanted = wanted > 0
    left = lax.all_gather(tile[None], "col", axis=0, tiled=True)

    far_index = band_index(m_ids[:, None], residue_ids[None, :], own_residue, slots)
    far_wide = widen(far, far_index, slots)
    left_index = band_index(
        m_ids[None, None, :], row_residues[None, :, None], order[:, None, None], slots
    )
    left_wide = widen(left, left_index, slots)
    tile_index = band_index(m_ids[None, :], row_residues[:, None], own_residue, slots)
    tile_high = (tile_index % (2 * slots)) >= slots

    def spread_mask(mask):
        return jnp.repeat(mask, BLOCK_EDGE, axis=-1)[:, :, None, :]

    def narrow(wide):
        chosen = jnp.where(spread_mask(tile_high), wide[..., lanes:], wide[..., :lanes])
        return jnp.where(spread_mask(wanted), chosen, 0.0)

    square = narrow(banded_product(left_wide, far_wide, order, False, slots)).astype(jnp.bfloat16)
    far_square = lax.all_gather(square, "row", axis=0, tiled=True)
    square_index = band_index(m_ids[None, :], order[:, None], own_residue, slots)
    square_wide = widen(far_square, square_index, slots)
    cube = narrow(banded_product(left_wide, square_wide, residue_ids, True, slots))
    stepped = (
        1.5 * tile.astype(jnp.float32) - 0.5 / (BLOCK_EDGE * band_extent) * cube
    ).astype(jnp.bfloat16)
    hit = (tile_index % panel_cols)[..., None] == m_ids
    target = jnp.sum(jnp.where(hit, inside, 0), axis=-1).astype(jnp.int32).reshape(-1)
    return spread(stepped, source, target, panel_cols)


def solution(mesh):
    return jax.shard_map(
        shards,
        mesh=mesh,
        in_specs=(P(("row", "col"), None, None), P(("row", "col"), None), P()),
        out_specs=P("row", "col"),
        check_vma=False,
    )
```

profile of v0, /device:TPU:3, one launch (start us, length us, event | category | flops | bytes accessed | tf_op | source)
XLA Modules:
  0.0 667.7 jit_solution(13469583311150154104)
XLA Ops:
  6.5 0.8 and_select_fusion
  8.4 2.0 fusion
  10.4 6.9 %reshape.322 = bf16[8,8,4,64,64]{4,3,0,2,1:T(8,128)(2,1)} reshape(bf16[8,8,4,4096]{3,0,2,1:T(8,128)(2,1)} %fusion) | data formatting | bytes 4194304 | tf_op jit(solution)/shard_map/reshape | solution.py:158
  17.3 12.4 %copy.23 = bf16[8,8,4,64,64]{4,2,3,1,0:T(4,128)(2,1)} copy(bf16[8,8,4,64,64]{4,3,0,2,1:T(8,128)(2,1)} %reshape.322) | data formatting | bytes 4194304 | tf_op jit(solution)/shard_map/reshape | solution.py:158
  29.8 6.0 reshape.323
  35.7 52.8 %all_to_all.5 = bf16[8,8,64,256]{3,2,1,0:T(8,128)(2,1)} all-to-all(bf16[8,8,64,256]{3,2,1,0:T(8,128)(2,1)S(1)} %reshape.323), channel_id=1, replica_groups=mesh['row'=4,'col'=8] {'col'}, dimensions={0} | all-to-all | bytes 4194304 | tf_op jit(solution)/shard_map/all_to_all | solution.py:162
  94.1 52.3 %all-gather.5.cloned.1.call-done = bf16[256,64,256]{2,1,0:T(8,128)(2,1)} async-done(((bf16[64,64,256]{2,1,0:T(8,128)(2,1)}), bf16[256,64,256]{2,1,0:T(8,128)(2,1)}) %all-gather.5.cloned.1.call-update) | async-done | bytes 8388624 | tf_op jit(solution)/shard_map/all_gather | solution.py:164
  146.4 1.7 dynamic-slice_bitcast_fusion.1
  148.2 1.7 pad_maximum_fusion.3
  150.4 0.7 broadcast_in_dim.193
  153.4 64.3 %all_gather.13 = bf16[256,32]{1,0:T(8,128)(2,1)S(1)} all-gather(bf16[8,32]{1,0:T(8,128)(2,1)S(1)} %copy.17), channel_id=1, replica_groups=mesh['row'=4,'col'=8] {'row','col'}, dimensions={0}, use_global_device_ids=true | all-gather | bytes 16896 | tf_op jit(solution)/shard_map/all_gather | solution.py:151
  219.2 4.5 broadcast_select_fusion.3
  223.8 6.7 %pad_maximum_fusion.1.far0.far1.far2.far3 = bf16[32,8,64,512]{3,2,1,0:T(8,128)(2,1)} fusion(bf16[32,8,64,256]{3,2,1,0:T(8,128)(2,1)S(1)} %get-tuple-element.14, bf16[32,8,64,256]{3,2,1,0:T(8,128)(2,1)S(1)} %get-tuple-element.13), kind=kLoop, calls=%fused_computation.1 | loop fusion | flops 33554432 | bytes 33554432 | tf_op jit(solution)/shard_map/concatenate | solution.py:107
  230.5 147.3 %all-gather.9.cloned.1.call-done = bf16[16,32,64,256]{3,2,1,0:T(8,128)(2,1)} async-done(((bf16[2,32,64,256]{3,2,1,0:T(8,128)(2,1)}), bf16[16,32,64,256]{3,2,1,0:T(8,128)(2,1)}) %all-gather.9.cloned.1.call-update) | async-done | bytes 16777232 | tf_op jit(solution)/shard_map/all_gather | solution.py:181
  377.8 18.3 %broadcast_select_fusion.1 = (bf16[8,2,32,64,256]{4,3,2,1,0:T(8,128)(2,1)}, bf16[8,2,32,64,256]{4,3,2,1,0:T(8,128)(2,1)}) fusion(bf16[8,2,32,64,256]{4,3,2,1,0:T(8,128)(2,1)} %bitcast.29, pred[8,2,32,256]{3,2,1,0:T(8,128)(4,1)S(1)} %broadcast_in_dim.194), kind=kLoop, calls=%fused_computation.4 | loop fusion | flops 16777216 | bytes 50462720 | tf_op jit(solution)/shard_map/jit(_where)/select_n | solution.py:108
  396.1 22.8 %pad_maximum_fusion.left_ref = bf16[8,2,32,64,512]{4,3,2,1,0:T(8,128)(2,1)} fusion(bf16[8,2,32,64,256]{4,3,2,1,0:T(8,128)(2,1)} %get-tuple-element.10, bf16[8,2,32,64,256]{4,3,2,1,0:T(8,128)(2,1)} %get-tuple-element.9), kind=kLoop, calls=%fused_computation | loop fusion | flops 67108864 | bytes 67108864 | tf_op jit(solution)/shard_map/concatenate | solution.py:107
  418.9 63.3 %shard_map.37 = f32[2,32,64,512]{3,2,1,0:T(8,128)} custom-call(s32[8]{0:T(128)} %copy-done.3, bf16[8,2,32,64,512]{4,3,2,1,0:T(8,128)(2,1)} %pad_maximum_fusion.left_ref, bf16[32,8,64,512]{3,2,1,0:T(8,128)(2,1)} %pad_maximum_fusion.1.far0.far1.far2.far3, bf16[32,8,64,512]{3,2,1,0:T(8,128)(2,1)} %pad_maximum_fusion.1.far0.far1.far2.far3, ...), custom_call_target="tpu_custom_call" | custom-call | tf_op jit(solution)/shard_map/pallas_call | solution.py:43
  482.2 6.4 fusion.6
  492.0 53.2 %all-gather.7.cloned.1.call-done = bf16[8,32,64,256]{3,2,1,0:T(8,128)(2,1)} async-done(((bf16[2,32,64,256]{3,2,1,0:T(8,128)(2,1)}), bf16[8,32,64,256]{3,2,1,0:T(8,128)(2,1)}) %all-gather.7.cloned.1.call-update) | async-done | bytes 8388624 | tf_op jit(solution)/shard_map/all_gather | solution.py:200
  545.2 4.5 broadcast_select_fusion.5
  549.7 6.7 %pad_maximum_fusion.2.far0.far1.far2.far3 = bf16[8,32,64,512]{3,2,1,0:T(8,128)(2,1)} fusion(bf16[8,32,64,256]{3,2,1,0:T(8,128)(2,1)S(1)} %get-tuple-element.12, bf16[8,32,64,256]{3,2,1,0:T(8,128)(2,1)S(1)} %get-tuple-element.11), kind=kLoop, calls=%fused_computation.2 | loop fusion | flops 33554432 | bytes 33554432 | tf_op jit(solution)/shard_map/concatenate | solution.py:107
  557.0 63.2 %shard_map.38 = f32[2,32,64,512]{3,2,1,0:T(8,128)} custom-call(s32[8]{0:T(128)} %iota.69.order_ref, bf16[8,2,32,64,512]{4,3,2,1,0:T(8,128)(2,1)} %pad_maximum_fusion.left_ref, bf16[8,32,64,512]{3,2,1,0:T(8,128)(2,1)} %pad_maximum_fusion.2.far0.far1.far2.far3, bf16[8,32,64,512]{3,2,1,0:T(8,128)(2,1)} %pad_maximum_fusion.2.far0.far1.far2.far3, ...), custom_call_target="tpu_custom_call" | custom-call | tf_op jit(solution)/shard_map/pallas_call | solution.py:43
  620.2 5.6 fusion.4.rows_ref
  625.8 35.3 %shard_map.39 = bf16[4096,2048]{1,0:T(8,128)(2,1)} custom-call(s32[32]{0:T(128)} %select_reduce_fusion.1.source_ref, s32[256]{0:T(256)} %reshape.321.target_ref, bf16[2,32,64,256]{3,2,1,0:T(8,128)(2,1)} %fusion.4.rows_ref), custom_call_target="tpu_custom_call" | custom-call | tf_op jit(solution)/shard_map/pallas_call | solution.py:79
  (65 shorter events, 11.2 us)
Async XLA Ops:
  6.5 1.9 copy-start
  6.5 139.9 %all-gather.5.cloned.1.call-start = ((), (), s32[]{:S(2)}) async-start(), calls=%async_computation.1 | async-start | bytes 10485760 | tf_op jit(solution)/shard_map/all_gather | solution.py:164
  7.5 142.4 %copy-start.3 = (s32[8]{0:T(128)}, s32[8]{0:T(128)S(1)}, u32[]{:S(2)}) copy-start(s32[8]{0:T(128)S(1)} %select_reduce_fusion.2.order_ref) | copy-start | bytes 100
  88.5 289.3 %all-gather.9.cloned.1.call-start = ((), (), s32[]{:S(2)}) async-start(), calls=%async_computation.3 | async-start | bytes 18874368 | tf_op jit(solution)/shard_map/all_gather | solution.py:181
  148.1 75.6 %copy-start.2 = (bf16[1,32,64,256]{3,2,1,0:T(8,128)(2,1)}, bf16[1,32,64,256]{3,2,1,0:T(8,128)(2,1)S(1)}, u32[]{:S(2)}) copy-start(bf16[1,32,64,256]{3,2,1,0:T(8,128)(2,1)S(1)} %get-tuple-element.16) | copy-start | bytes 3145732
  149.8 395.4 %all-gather.7.cloned.1.call-start = ((), (), s32[]{:S(2)}) async-start(), calls=%async_computation.2 | async-start | bytes 10485760 | tf_op jit(solution)/shard_map/all_gather | solution.py:200
  482.2 6.4 copy-start.5
  482.2 6.6 copy-start.4
  620.2 40.9 %copy-start.1 = (bf16[8,32,4096]{2,1,0:T(8,128)(2,1)S(1)}, bf16[8,32,4096]{2,1,0:T(8,128)(2,1)}, u32[]{:S(2)}) copy-start(bf16[8,32,4096]{2,1,0:T(8,128)(2,1)} %param.3) | copy-start | bytes 6291460
Sparse Core Ops, SparseCore 0:
  88.6 57.7 all-gather.4
  150.0 227.8 all-gather.8
  488.7 56.4 all-gather.6
where the time goes:
time: 677 us; the launch traced here: 668 us
  waiting for transfers between devices  253 us (37%)
  Pallas kernels  162 us (24%)
  blocking collectives  117 us (17%)
  other arithmetic  83.2 us (12%)
  local copies, waits for them, and re-layouts  33.6 us (5%)
  between operations  17 us (3%)
    all_gather x1, waiting for transfers between devices, shards(): left = lax.all_gather(tile[None], 'col', axis=0, tiled=True)  147 us
    pallas_call x2, Pallas kernels, banded_product(): pl.pallas_call(multiply_kernel, out_shape=jax.ShapeDtypeStruct((halves, c...  126 us
    all_gather x1, blocking collectives, shards(): lax.all_gather(kept.reshape(local_rows, panels * slots), ('row', 'col'),...  64.3 us
    all_gather x1, waiting for transfers between devices, shards(): far_square = lax.all_gather(square, 'row', axis=0, tiled=True)  53.2 us
    all_to_all x1, blocking collectives, shards(): lax.all_to_all(values, 'col', split_axis=0, concat_axis=0, tiled=True)  52.8 us
    all_gather x1, waiting for transfers between devices, shards(): lax.all_gather(first, 'row', axis=0, tiled=True)  52.3 us
    concatenate x3, other arithmetic, widen(): jnp.concatenate([jnp.where(high, zero, values), jnp.where(high, values, z...  36.2 us
    pallas_call x1, Pallas kernels, spread(): pl.pallas_call(spread_kernel, out_shape=jax.ShapeDtypeStruct((halves * co...  35.3 us
  transfers between devices with their start and end apart: 3, of which 3 were waited for; matrix products, arithmetic and copies ran while one was open for 3% of the time, Pallas kernels for 0%

commit v1 on v0

--- a/solution.py
+++ b/solution.py
@@ -1,3 +1,5 @@
+import functools
+
 import jax
 import jax.numpy as jnp
 from jax import lax
@@ -6,6 +8,8 @@
 from jax.sharding import PartitionSpec as P
 
 BLOCK_EDGE = 64
+MESH = pl.DeviceIdType.MESH
+ANY = pl.BlockSpec(memory_space=pl.ANY)
 
 
 def multiply_kernel(order_ref, left_ref, far0, far1, far2, far3, out_ref):
@@ -109,7 +113,7 @@
     )
 
 
-def shards(x_vals, occupancy, perm):
+def panel_shards(x_vals, occupancy, perm):
     row_devices = lax.axis_size("row")
     panels = lax.axis_size("col")
     own_row = lax.axis_index("row")
@@ -209,6 +213,505 @@
     return spread(stepped, source, target, panel_cols)
 
 
+class Place:
+    def __init__(self, panels):
+        self.depth = panels // 2
+        self.quarter = panels // 4
+        row, col = lax.axis_index("row"), lax.axis_index("col")
+        self.half, self.core = row // 2, row % 2
+        self.level, self.lane = col // 2, col % 2
+        self.step = jnp.where(self.half == 0, self.level, self.depth - 1 - self.level)
+        self.ring = self.half * self.depth + self.step
+
+    def device(self, half, core, level, lane):
+        return (2 * half + core, 2 * level + lane)
+
+    def at_ring(self, ring):
+        half = ring // self.depth
+        step = ring % self.depth
+        level = jnp.where(half == 0, step, self.depth - 1 - step)
+        return self.device(half, self.core, level, self.lane)
+
+    def neighbour(self, by):
+        return self.at_ring((self.ring + by + 2 * self.depth) % (2 * self.depth))
+
+    def group_target(self):
+        step = self.core * self.quarter + self.level // 2
+        level = jnp.where(self.half == 0, step, self.depth - 1 - step)
+        return self.device(self.half, 1 - self.level % 2, level, self.lane)
+
+    def group_source(self):
+        level = 2 * (self.step % self.quarter) + 1 - self.core
+        return self.device(self.half, self.step // self.quarter, level, self.lane)
+
+
+def greet(devices):
+    barrier = pltpu.get_barrier_semaphore()
+    for device in devices:
+        pl.semaphore_signal(barrier, inc=1, device_id=device, device_id_type=MESH)
+    pl.semaphore_wait(barrier, len(devices))
+
+
+def remote(source, target, send, recv, device):
+    return pltpu.make_async_remote_copy(
+        src_ref=source,
+        dst_ref=target,
+        send_sem=send,
+        recv_sem=recv,
+        device_id=device,
+        device_id_type=MESH,
+    )
+
+
+def gather_kernel(panels, rows, marks, all_rows, all_marks, *sems):
+    place = Place(panels)
+    count = rows.shape[0]
+    over_level, over_lane, over_core, relayed = [sems[2 * n : 2 * n + 2] for n in range(4)]
+    target, source = place.group_target(), place.group_source()
+    lane_peer = place.device(place.half, place.core, place.level, 1 - place.lane)
+    core_peer = place.device(place.half, 1 - place.core, place.level, place.lane)
+    target_slot = 2 * (place.level % 2) + place.lane
+    own_slot = 2 * (1 - place.core) + place.lane
+    peer_slot = 2 * (1 - place.core) + 1 - place.lane
+    greet((source, lane_peer, core_peer))
+
+    def piece(slot, n):
+        return all_marks.at[slot] if n == 0 else all_rows.at[slot, n - 1]
+
+    def copies(sem, device, slot, first=False):
+        out = []
+        for n in range(count + 1):
+            origin = (marks if n == 0 else rows.at[n - 1]) if first else piece(slot, n)
+            out.append(remote(origin, piece(slot, n), sem[0].at[n], sem[1].at[n], device))
+        return out
+
+    moves = copies(over_level, target, target_slot, True)
+    lanes = copies(over_lane, lane_peer, own_slot)
+    cores = copies(over_core, core_peer, own_slot)
+    relays = copies(relayed, core_peer, peer_slot)
+    for move in moves:
+        move.start()
+    for move, lane, core in zip(moves, lanes, cores):
+        move.wait_recv()
+        lane.start()
+        core.start()
+    for lane, relay in zip(lanes, relays):
+        lane.wait_recv()
+        relay.start()
+    for core, relay in zip(cores, relays):
+        core.wait_recv()
+        relay.wait_recv()
+    for group in (moves, lanes, cores, relays):
+        for copy in group:
+            copy.wait_send()
+
+
+def gather_groups(rows, marks, panels):
+    count = rows.shape[0]
+    sems = [pltpu.SemaphoreType.DMA((count + 1,)) for _ in range(8)]
+    return pl.pallas_call(
+        functools.partial(gather_kernel, panels),
+        out_shape=(
+            jax.ShapeDtypeStruct((4,) + rows.shape, rows.dtype),
+            jax.ShapeDtypeStruct((4,) + marks.shape, marks.dtype),
+        ),
+        in_specs=[ANY, ANY],
+        out_specs=(ANY, ANY),
+        scratch_shapes=sems,
+        compiler_params=pltpu.CompilerParams(collective_id=0, has_side_effects=True),
+        name="gather_groups",
+    )(rows, marks)
+
+
+def lay_kernel(rows_ref, marks_ref, pick_ref, left_ref, right_ref, kept_ref):
+    count, edge, lanes = rows_ref.shape[1:]
+    octet = count * edge
+    rest = left_ref.shape[-1] - lanes
+    for t in range(count):
+        row = rows_ref[0, t]
+        parts = [row]
+        if t:
+            parts = [jnp.zeros((edge, t * edge), row.dtype)] + parts
+        if rest - t * edge:
+            parts = parts + [jnp.zeros((edge, rest - t * edge), row.dtype)]
+        left_ref[0, t * edge : (t + 1) * edge, :] = jnp.concatenate(parts, axis=1)
+    pick = pick_ref[...]
+    width = pick.shape[1]
+    for o in range(left_ref.shape[-1] // octet):
+        at, to = slice(o * octet, (o + 1) * octet), slice(o * width, (o + 1) * width)
+        right_ref[0, :, to] = jnp.dot(
+            left_ref[0, :, at], pick, preferred_element_type=jnp.float32
+        ).astype(right_ref.dtype)
+        kept_ref[0, :, to] = jnp.dot(
+            marks_ref[0, :, at], pick, preferred_element_type=jnp.float32
+        )
+
+
+def lay_out(rows, marks, pick):
+    groups, count, edge, lanes = rows.shape
+    octet, width = pick.shape
+    wide = marks.shape[-1]
+    narrow = wide // octet * width
+    return pl.pallas_call(
+        lay_kernel,
+        out_shape=(
+            jax.ShapeDtypeStruct((groups, octet, wide), rows.dtype),
+            jax.ShapeDtypeStruct((groups + 4, octet, narrow), rows.dtype),
+            jax.ShapeDtypeStruct((groups, count, narrow), jnp.float32),
+        ),
+        grid=(groups,),
+        in_specs=[
+            pl.BlockSpec((1, count, edge, lanes), lambda g: (g, 0, 0, 0)),
+            pl.BlockSpec((1, count, wide), lambda g: (g, 0, 0)),
+            pl.BlockSpec((octet, width), lambda g: (0, 0)),
+        ],
+        out_specs=(
+            pl.BlockSpec((1, octet, wide), lambda g: (g, 0, 0)),
+            pl.BlockSpec((1, octet, narrow), lambda g: (g + 2, 0, 0)),
+            pl.BlockSpec((1, count, narrow), lambda g: (g, 0, 0)),
+        ),
+        compiler_params=pltpu.CompilerParams(dimension_semantics=("arbitrary",)),
+        name="lay_out",
+    )(rows, marks, pick)
+
+
+def halo_kernel(panels, tiles_in, tiles, send, recv):
+    del tiles_in
+    place = Place(panels)
+    after, before = place.neighbour(1), place.neighbour(-1)
+    groups = tiles.shape[0] - 4
+    wide = tiles.shape[-1]
+    step = wide // 5
+    greet((after, before))
+    moves = (
+        (groups, 0, slice(2 * step, wide), after),
+        (groups + 1, 1, slice(step, wide), after),
+        (2, groups + 2, slice(0, 4 * step), before),
+        (3, groups + 3, slice(0, 3 * step), before),
+    )
+    copies = [
+        remote(
+            tiles.at[origin, :, lanes], tiles.at[to, :, lanes], send.at[n], recv.at[n], device
+        )
+        for n, (origin, to, lanes, device) in enumerate(moves)
+    ]
+    for copy in copies:
+        copy.start()
+    for copy in copies:
+        copy.wait()
+
+
+def exchange_halo(tiles, panels, collective_id):
+    return pl.pallas_call(
+        functools.partial(halo_kernel, panels),
+        out_shape=jax.ShapeDtypeStruct(tiles.shape, tiles.dtype),
+        in_specs=[ANY],
+        out_specs=ANY,
+        scratch_shapes=[pltpu.SemaphoreType.DMA((4,)), pltpu.SemaphoreType.DMA((4,))],
+        input_output_aliases={0: 0},
+        compiler_params=pltpu.CompilerParams(
+            collective_id=collective_id, has_side_effects=True
+        ),
+        name="exchange_halo",
+    )(tiles)
+
+
+def multiply(left_ref, tiles_ref, total):
+    t = pl.program_id(0)
+    depth, wide = tiles_ref.shape[1:]
+    step = wide // 5
+    for n, (at, to) in enumerate(((0, 0), (-1, 0), (-2, 0), (1, 1), (2, 2))):
+        reach = wide - abs(at) * step
+        first = 0 if at >= 0 else wide - reach
+        tile = tiles_ref[t + 2 + at, :, first : first + reach]
+        update = jnp.dot(
+            left_ref[0, :, (2 + at) * depth : (3 + at) * depth],
+            tile,
+            preferred_element_type=jnp.float32,
+        )
+        if n == 0:
+            total[...] = update
+        else:
+            total[:, to * step : to * step + reach] += update
+
+
+def square_kernel(left_ref, tiles_ref, kept_ref, out_ref, total):
+    multiply(left_ref, tiles_ref, total)
+    count = kept_ref.shape[1]
+    edge = total.shape[0] // count
+    for r in range(count):
+        at = slice(r * edge, (r + 1) * edge)
+        out_ref[0, at, :] = (total[at, :] * kept_ref[0, r : r + 1, :]).astype(out_ref.dtype)
+
+
+def square_tiles(left, tiles, kept):
+    groups, octet, wide = left.shape
+    narrow = tiles.shape[-1]
+    return pl.pallas_call(
+        square_kernel,
+        out_shape=jax.ShapeDtypeStruct(tiles.shape, tiles.dtype),
+        grid=(groups,),
+        in_specs=[
+            pl.BlockSpec((1, octet, wide), lambda g: (g, 0, 0)),
+            pl.BlockSpec(tiles.shape, lambda g: (0, 0, 0)),
+            pl.BlockSpec((1,) + kept.shape[1:], lambda g: (g, 0, 0)),
+        ],
+        out_specs=pl.BlockSpec((1, octet, narrow), lambda g: (g + 2, 0, 0)),
+        scratch_shapes=[pltpu.VMEM((octet, narrow), jnp.float32)],
+        compiler_params=pltpu.CompilerParams(dimension_semantics=("arbitrary",)),
+        name="square_tiles",
+    )(left, tiles, kept)
+
+
+def step_kernel(
+    scale, residues, order, left_ref, tiles_ref, own_ref, kept_ref, out_ref, total
+):
+    multiply(left_ref, tiles_ref, total)
+    count = kept_ref.shape[1]
+    edge = total.shape[0] // count
+    for r in range(count):
+        at = slice(r * edge, (r + 1) * edge)
+        total[at, :] = 1.5 * own_ref[0, at, :].astype(jnp.float32) - scale * (
+            total[at, :] * kept_ref[0, r : r + 1, :]
+        )
+    row_devices, pair, halves = out_ref.shape[:3]
+    lanes = 2 * edge
+    slots = out_ref.shape[-1] // edge
+    low = lax.broadcasted_iota(jnp.int32, (edge, lanes), 1) < edge
+    for dest in range(row_devices):
+        for e in range(halves):
+            row = order[dest * halves + e]
+            at = pl.ds(pl.multiple_of(row * edge, edge), edge)
+            for h in range(pair):
+                late = (residues[h] < row).astype(jnp.int32)
+                for w in range(slots // 2):
+                    start = pl.multiple_of((late + 2 * w) * lanes, lanes)
+                    one = total[at, pl.ds(start, lanes)]
+                    two = total[at, pl.ds(pl.multiple_of(start + lanes, lanes), lanes)]
+                    if h == 0:
+                        two = pltpu.roll(two, edge, 1)
+                    else:
+                        one = pltpu.roll(one, edge, 1)
+                    out_ref[dest, h, e, 0, :, w * lanes : (w + 1) * lanes] = jnp.where(
+                        low, one, two
+                    ).astype(out_ref.dtype)
+
+
+def step_tiles(left, tiles, own, kept, residues, order, row_devices, scale):
+    groups, octet, wide = left.shape
+    narrow = tiles.shape[-1]
+    count = kept.shape[1]
+    edge = octet // count
+    halves = count // row_devices
+    out = (row_devices, 2, halves, groups, edge, 4 * edge)
+    return pl.pallas_call(
+        functools.partial(step_kernel, scale),
+        out_shape=jax.ShapeDtypeStruct(out, tiles.dtype),
+        grid_spec=pltpu.PrefetchScalarGridSpec(
+            num_scalar_prefetch=2,
+            grid=(groups,),
+            in_specs=[
+                pl.BlockSpec((1, octet, wide), lambda g, *_: (g, 0, 0)),
+                pl.BlockSpec(tiles.shape, lambda g, *_: (0, 0, 0)),
+                pl.BlockSpec((1, octet, narrow), lambda g, *_: (g + 2, 0, 0)),
+                pl.BlockSpec((1,) + kept.shape[1:], lambda g, *_: (g, 0, 0)),
+            ],
+            out_specs=pl.BlockSpec(
+                out[:3] + (1,) + out[4:], lambda g, *_: (0, 0, 0, g, 0, 0)
+            ),
+            scratch_shapes=[pltpu.VMEM((octet, narrow), jnp.float32)],
+        ),
+        compiler_params=pltpu.CompilerParams(dimension_semantics=("arbitrary",)),
+        name="step_tiles",
+    )(residues, order, left, tiles, own, kept)
+
+
+def deliver_kernel(panels, packed, out, send, recv, local):
+    place = Place(panels)
+    row_devices, pair = packed.shape[:2]
+    supers = out.shape[0]
+    row, col = lax.axis_index("row"), lax.axis_index("col")
+    owner = place.level // 2
+    sources = []
+    for ring in range(supers):
+        half, step = ring // place.depth, ring % place.depth
+        level = step if half == 0 else place.depth - 1 - step
+        sources.append((2 * half + owner, 2 * level + place.lane))
+    targets = [
+        (dest, 2 * (2 * place.core + h) + place.lane)
+        for dest in range(row_devices)
+        for h in range(pair)
+    ]
+    barrier = pltpu.get_barrier_semaphore()
+    for source in sources:
+
+        @pl.when(jnp.logical_or(source[0] != row, source[1] != col))
+        def _(source=source):
+            pl.semaphore_signal(barrier, inc=1, device_id=source, device_id_type=MESH)
+
+    own = place.level // 2 == place.core
+    pl.semaphore_wait(barrier, jnp.where(own, len(targets) - 1, len(targets)))
+
+    def each(act_remote, act_local):
+        for n, target in enumerate(targets):
+            here = jnp.logical_and(target[0] == row, target[1] == col)
+            dest, h = n // pair, n % pair
+
+            @pl.when(here)
+            def _(dest=dest, h=h):
+                act_local(
+                    pltpu.make_async_copy(packed.at[dest, h], out.at[place.ring], local)
+                )
+
+            @pl.when(jnp.logical_not(here))
+            def _(dest=dest, h=h, n=n, target=target):
+                act_remote(
+                    remote(
+                        packed.at[dest, h],
+                        out.at[place.ring],
+                        send.at[n],
+                        recv.at[place.ring],
+                        target,
+                    )
+                )
+
+    each(lambda c: c.start(), lambda c: c.start())
+    for n, source in enumerate(sources):
+
+        @pl.when(jnp.logical_or(source[0] != row, source[1] != col))
+        def _(n=n, source=source):
+            remote(packed.at[0, 0], out.at[n], send.at[0], recv.at[n], source).wait_recv()
+
+    each(lambda c: c.wait_send(), lambda c: c.wait())
+
+
+def deliver(packed, panels, supers):
+    return pl.pallas_call(
+        functools.partial(deliver_kernel, panels),
+        out_shape=jax.ShapeDtypeStruct((supers,) + packed.shape[2:], packed.dtype),
+        in_specs=[ANY],
+        out_specs=ANY,
+        scratch_shapes=[
+            pltpu.SemaphoreType.DMA((packed.shape[0] * packed.shape[1],)),
+            pltpu.SemaphoreType.DMA((supers,)),
+            pltpu.SemaphoreType.DMA,
+        ],
+        compiler_params=pltpu.CompilerParams(collective_id=3, has_side_effects=True),
+        name="deliver",
+    )(packed)
+
+
+def place_kernel(inside, source, late, parts_ref, out_ref):
+    supers, halves, groups, edge, width = parts_ref.shape
+    count = supers * groups
+    lanes = 2 * edge
+    rows = out_ref.shape[0] // edge
+    half = lax.broadcasted_iota(jnp.int32, (edge, lanes), 1) // edge
+    first = pl.program_id(0) * rows
+    e = first // count
+    out_ref[...] = jnp.zeros_like(out_ref)
+
+    @pl.loop(0, rows)
+    def _(n):
+        origin = source[lax.rem(first + n, count)]
+        at = pl.ds(pl.multiple_of(n * edge, edge), edge)
+        base = origin - 2 + late[e] + count
+        for w in range(width // lanes):
+            tile = parts_ref[
+                origin // groups, e, lax.rem(origin, groups), :, w * lanes : (w + 1) * lanes
+            ].astype(jnp.float32)
+            rolled = pltpu.roll(tile, edge, 1)
+            for side in range(2):
+                block = inside[lax.rem(base + 2 * w + side, count)]
+                odd = lax.rem(block, 2)
+                value = jnp.where(odd == side, tile, rolled)
+                value = jnp.where(half == odd, value, 0.0).astype(out_ref.dtype)
+                to = pl.ds(pl.multiple_of((block // 2) * lanes, lanes), lanes)
+                out_ref[at, to] += value
+
+
+def place_blocks(parts, inside, source, late):
+    supers, halves, groups, edge, width = parts.shape
+    count = supers * groups
+    rows = min(count, 8)
+    return pl.pallas_call(
+        place_kernel,
+        out_shape=jax.ShapeDtypeStruct((halves * count * edge, count * edge), parts.dtype),
+        grid_spec=pltpu.PrefetchScalarGridSpec(
+            num_scalar_prefetch=3,
+            grid=(halves * count // rows,),
+            in_specs=[pl.BlockSpec(parts.shape, lambda g, *_: (0, 0, 0, 0, 0))],
+            out_specs=pl.BlockSpec((rows * edge, count * edge), lambda g, *_: (g, 0)),
+        ),
+        compiler_params=pltpu.CompilerParams(dimension_semantics=("arbitrary",)),
+        name="place_blocks",
+    )(inside, source, late, parts)
+
+
+def band_shards(x_vals, occupancy, perm):
+    row_devices = lax.axis_size("row")
+    panels = lax.axis_size("col")
+    own_row, own_col = lax.axis_index("row"), lax.axis_index("col")
+    count, band, area = x_vals.shape
+    block_count = perm.shape[0]
+    panel_cols = block_count // panels
+    halves = panels // row_devices
+    edge = BLOCK_EDGE
+    wide = band + count
+
+    ids = jnp.arange(panels, dtype=jnp.int32)
+    spots = perm[:panels] // panel_cols
+    order = jnp.sum(jnp.where(spots[None, :] == ids[:, None], ids[None, :], 0), axis=1)
+    order = order.astype(jnp.int32)
+    inside = (perm[::panels] % panel_cols).astype(jnp.int32)
+    m_ids = jnp.arange(panel_cols, dtype=jnp.int32)
+    source = jnp.sum(
+        jnp.where(inside[None, :] == m_ids[:, None], m_ids[None, :], 0), axis=1
+    ).astype(jnp.int32)
+    lane, core = own_col % 2, own_row % 2
+    mine = jnp.arange(2, dtype=jnp.int32)
+    residues = order[2 * (2 * core + mine) + lane]
+    late = (
+        order[own_col] < lax.dynamic_slice_in_dim(order, own_row * halves, halves)
+    ).astype(jnp.int32)
+
+    lane_ids = jnp.arange(2 * edge, dtype=jnp.int32)
+    wanted = jnp.where(lane_ids < edge, residues[0], residues[1]) * edge + lane_ids % edge
+    pick = (jnp.arange(panels * edge, dtype=jnp.int32)[:, None] == wanted[None, :]).astype(
+        x_vals.dtype
+    )
+    present = occupancy == 1
+    rows = jnp.where(present[:, :, None], x_vals, jnp.zeros((), x_vals.dtype))
+    rows = (
+        rows.reshape(count, band, edge, edge)
+        .transpose(0, 2, 1, 3)
+        .reshape(count, edge, band * edge)
+    )
+    spot = jnp.arange(wide, dtype=jnp.int32)[None, :] - jnp.arange(count, dtype=jnp.int32)[:, None]
+    hit = spot[:, :, None] == jnp.arange(band, dtype=jnp.int32)
+    marks = jnp.any(hit & present[:, None, :], axis=2)
+    marks = jnp.repeat(marks.astype(x_vals.dtype), edge, axis=1)
+
+    all_rows, all_marks = gather_groups(rows, marks, panels)
+    left, tiles, kept = lay_out(all_rows, all_marks, pick)
+    tiles = exchange_halo(tiles, panels, 1)
+    square = exchange_halo(square_tiles(left, tiles, kept), panels, 2)
+    packed = step_tiles(
+        left, square, tiles, kept, residues, order, row_devices, 0.5 / (edge * band)
+    )
+    parts = deliver(packed, panels, block_count // (4 * count))
+    return place_blocks(parts, inside, source, late)
+
+
+def shards(x_vals, occupancy, perm):
+    row_devices = lax.axis_size("row")
+    panels = lax.axis_size("col")
+    count, band, _ = x_vals.shape
+    if row_devices == 4 and panels == count == 2 * row_devices and band == 4 * count:
+        return band_shards(x_vals, occupancy, perm)
+    return panel_shards(x_vals, occupancy, perm)
+
+
 def solution(mesh):
     return jax.shard_map(
         shards,

time: 677 us -> 237 us (0.35); the launches traced: 668 us -> 234 us
  waiting for transfers between devices: 253 us -> 0 us
  blocking collectives: 117 us -> 0 us
  other arithmetic: 83.2 us -> 7.48 us
  Pallas kernels: 162 us -> 204 us
  between operations: 17 us -> 0.09 us
  local copies, waits for them, and re-layouts: 33.6 us -> 22.6 us
    all_gather x3 -> x0, waiting for transfers between devices: 253 us -> none  [the longest x1 147 us: shards(): left = lax.all_gather(tile[None], 'col', axis=0, tiled=True)]
    all_gather x1 -> x0, blocking collectives: 64.3 us -> none  [shards(): lax.all_gather(kept.reshape(local_rows, panels * slots), ('row', 'col'),...]
    all_to_all x1 -> x0, blocking collectives: 52.8 us -> none  [shards(): lax.all_to_all(values, 'col', split_axis=0, concat_axis=0, tiled=True)]
    pallas_call x3 -> x8, Pallas kernels: 162 us -> 204 us  [the longest x1 60.9 us: gather_groups(): pl.pallas_call(functools.partial(gather_kernel, panels), out_shape=(jax.S...]
    concatenate x3 -> x0, other arithmetic: 36.2 us -> none  [widen(): jnp.concatenate([jnp.where(high, zero, values), jnp.where(high, values, z...]
    select_n x7 -> x4, other arithmetic: 28.3 us -> 2.5 us  [the longest x1 1.79 us: band_shards(): rows = jnp.where(present[:, :, None], x_vals, jnp.zeros((), x_vals.dtype))]
    convert_element_type x6 -> x3, other arithmetic: 14 us -> 2.01 us  [the longest x1 1.31 us: band_shards(): late = (order[own_col] < lax.dynamic_slice_in_dim(order, own_row * halves...]
    reshape x6 -> x4, local copies, waits for them, and re-layouts: 26.4 us -> 19.8 us  [the longest x2 12.4 us: band_shards(): rows.reshape(count, band, edge, edge).transpose(0, 2, 1, 3)]
  transfers between devices with their start and end apart: 3 -> 0, of which waited for: 3 -> 0; matrix products, arithmetic and copies ran while one was open for 3% -> 0% of each run, Pallas kernels for 0% -> 0%
where the time goes in v1:
time: 237 us; the launch traced here: 234 us
  Pallas kernels  204 us (86%)
  local copies, waits for them, and re-layouts  22.6 us (10%)
  other arithmetic  7.48 us (3%)
    pallas_call x1, Pallas kernels, gather_groups(): pl.pallas_call(functools.partial(gather_kernel, panels), out_shape=(jax.S...  60.9 us
    pallas_call x1, Pallas kernels, deliver(): pl.pallas_call(functools.partial(deliver_kernel, panels), out_shape=jax.S...  50.6 us
    pallas_call x2, Pallas kernels, exchange_halo(): pl.pallas_call(functools.partial(halo_kernel, panels), out_shape=jax.Shap...  46 us
    pallas_call x1, Pallas kernels, step_tiles(): pl.pallas_call(functools.partial(step_kernel, scale), out_shape=jax.Shape...  13.1 us
    pallas_call x1, Pallas kernels, place_blocks(): pl.pallas_call(place_kernel, out_shape=jax.ShapeDtypeStruct((halves * cou...  12.9 us
    reshape x2, local copies, waits for them, and re-layouts, band_shards(): rows.reshape(count, band, edge, edge).transpose(0, 2, 1, 3)  12.4 us
    pallas_call x1, Pallas kernels, square_tiles(): pl.pallas_call(square_kernel, out_shape=jax.ShapeDtypeStruct(tiles.shape,...  11.3 us
    pallas_call x1, Pallas kernels, lay_out(): pl.pallas_call(lay_kernel, out_shape=(jax.ShapeDtypeStruct((groups, octet...  9.49 us

profile of v1, /device:TPU:3, one launch (start us, length us, event | category | flops | bytes accessed | tf_op | source)
XLA Modules:
  0.0 234.4 jit_solution(495226125174864533)
XLA Ops:
  0.0 0.7 and_select_fusion.1
  0.7 0.1 select_reduce_fusion.1.order
  0.8 0.6 dynamic_slice.6
  1.4 1.3 compare_convert_fusion.late
  2.7 0.8 slice.12
  3.5 0.7 select_reduce_fusion.source
  4.2 0.7 broadcast_compare_fusion
  4.9 0.6 gather_fusion
  5.6 0.7 fusion.7
  6.2 1.3 fusion.3
  7.8 0.7 reshape.63.marks
  8.6 0.7 fusion.pick_ref
  9.3 1.8 broadcast_select_fusion
  11.1 5.5 %reshape.61 = bf16[8,32,64,64]{3,2,1,0:T(8,128)(2,1)} reshape(bf16[8,32,4096]{2,1,0:T(8,128)(2,1)S(1)} %broadcast_select_fusion) | data formatting | bytes 4194304 | tf_op jit(solution)/shard_map/reshape | solution.py:686
  16.6 6.8 %copy.10 = bf16[8,32,64,64]{3,1,2,0:T(8,128)(2,1)} copy(bf16[8,32,64,64]{3,2,1,0:T(8,128)(2,1)} %reshape.61) | data formatting | bytes 4194304 | tf_op jit(solution)/shard_map/reshape | solution.py:686
  23.4 6.7 %reshape.62.rows = bf16[8,64,2048]{2,1,0:T(8,128)(2,1)} reshape(bf16[8,64,32,64]{3,2,1,0:T(8,128)(2,1)} %bitcast.10) | data formatting | bytes 4194304 | tf_op jit(solution)/shard_map/reshape | solution.py:688
  30.2 60.9 %gather_groups.1 = (bf16[4,8,64,2048]{3,2,1,0:T(8,128)(2,1)}, bf16[4,8,2560]{2,1,0:T(8,128)(2,1)}) custom-call(bf16[8,64,2048]{2,1,0:T(8,128)(2,1)} %reshape.62.rows, bf16[8,2560]{1,0:T(8,128)(2,1)} %reshape.63.marks), custom_call_target="tpu_custom_call" | custom-call | tf_op jit(solution)/shard_map/gather_groups/pallas_call | solution.py:312
  91.1 9.5 %lay_out.1 = (bf16[4,512,2560]{2,1,0:T(8,128)(2,1)}, bf16[8,512,640]{2,1,0:T(8,128)(2,1)}, f32[4,8,640]{2,1,0:T(8,128)}) custom-call(bf16[4,8,64,2048]{3,2,1,0:T(8,128)(2,1)} %get-tuple-element.10.rows_ref, bf16[4,8,2560]{2,1,0:T(8,128)(2,1)} %get-tuple-element.11.marks_ref, bf16[512,128]{1,0:T(8,128)(2,1)} %fusion.pick_ref), custom_call_target="tpu_custom_call" | custom-call | tf_op jit(solution)/shard_map/lay_out/pallas_call | solution.py:355
  100.6 22.2 %exchange_halo.2.tiles_ref.own_ref = bf16[8,512,640]{2,1,0:T(8,128)(2,1)} custom-call(bf16[8,512,640]{2,1,0:T(8,128)(2,1)} %get-tuple-element.13.tiles_in), custom_call_target="tpu_custom_call", output_to_operand_aliasing={{}: (0, {})} | custom-call | tf_op jit(solution)/shard_map/exchange_halo/pallas_call | solution.py:405
  122.8 11.3 %square_tiles.1.tiles_in = bf16[8,512,640]{2,1,0:T(8,128)(2,1)} custom-call(bf16[4,512,2560]{2,1,0:T(8,128)(2,1)} %get-tuple-element.12.left_ref, bf16[8,512,640]{2,1,0:T(8,128)(2,1)} %exchange_halo.2.tiles_ref.own_ref, f32[4,8,640]{2,1,0:T(8,128)} %get-tuple-element.14.kept_ref), custom_call_target="tpu_custom_call" | custom-call | tf_op jit(solution)/shard_map/square_tiles/pallas_call | solution.py:450
  134.1 23.8 %exchange_halo.3.tiles_ref = bf16[8,512,640]{2,1,0:T(8,128)(2,1)} custom-call(bf16[8,512,640]{2,1,0:T(8,128)(2,1)} %square_tiles.1.tiles_in), custom_call_target="tpu_custom_call", output_to_operand_aliasing={{}: (0, {})} | custom-call | tf_op jit(solution)/shard_map/exchange_halo/pallas_call | solution.py:405
  157.9 13.1 %step_tiles.1.packed = bf16[4,2,2,4,64,256]{5,4,3,2,1,0:T(8,128)(2,1)} custom-call(s32[2]{0:T(128)} %copy-done.1, s32[8]{0:T(128)} %copy-done, bf16[4,512,2560]{2,1,0:T(8,128)(2,1)} %get-tuple-element.12.left_ref, bf16[8,512,640]{2,1,0:T(8,128)(2,1)} %exchange_halo.3.tiles_ref, bf16[8,512,640]{2,1,0:T(8,128)(2,1)} %exchange_halo.2.tiles_ref.own_ref, ...), custom_call_target="tpu_custom_call" | custom-call | tf_op jit(solution)/shard_map/step_tiles/pallas_call | solution.py:507
  171.0 50.6 %deliver.1.parts_ref = bf16[8,2,4,64,256]{4,3,2,1,0:T(8,128)(2,1)} custom-call(bf16[4,2,2,4,64,256]{5,4,3,2,1,0:T(8,128)(2,1)} %step_tiles.1.packed), custom_call_target="tpu_custom_call" | custom-call | tf_op jit(solution)/shard_map/deliver/pallas_call | solution.py:589
  221.6 12.9 %place_blocks.1 = bf16[4096,2048]{1,0:T(8,128)(2,1)} custom-call(s32[32]{0:T(128)} %copy-done.2, s32[32]{0:T(128)} %select_reduce_fusion.source, s32[2]{0:T(128)} %compare_convert_fusion.late, bf16[8,2,4,64,256]{4,3,2,1,0:T(8,128)(2,1)} %deliver.1.parts_ref), custom_call_target="tpu_custom_call" | custom-call | tf_op jit(solution)/shard_map/place_blocks/pallas_call | solution.py:637
  (13 shorter events, 0.3 us)
Async XLA Ops:
  0.8 15.8 %copy-start = (s32[8]{0:T(128)}, s32[8]{0:T(128)S(1)}, u32[]{:S(2)}) copy-start(s32[8]{0:T(128)S(1)} %select_reduce_fusion.1.order) | copy-start | bytes 100
  3.5 13.1 %copy-start.2 = (s32[32]{0:T(128)}, s32[32]{0:T(128)S(1)}, u32[]{:S(2)}) copy-start(s32[32]{0:T(128)S(1)} %and_select_fusion.2.inside) | copy-start | bytes 388
  5.6 11.0 %copy-start.1 = (s32[2]{0:T(128)}, s32[2]{0:T(128)S(1)}, u32[]{:S(2)}) copy-start(s32[2]{0:T(128)S(1)} %gather_fusion) | copy-start | bytes 28

commit v2 on v0

--- a/solution.py
+++ b/solution.py
@@ -1,3 +1,5 @@
+import functools
+
 import jax
 import jax.numpy as jnp
 from jax import lax
@@ -6,6 +8,8 @@
 from jax.sharding import PartitionSpec as P
 
 BLOCK_EDGE = 64
+MESH = pl.DeviceIdType.MESH
+ANY = pl.BlockSpec(memory_space=pl.ANY)
 
 
 def multiply_kernel(order_ref, left_ref, far0, far1, far2, far3, out_ref):
@@ -109,7 +113,7 @@
     )
 
 
-def shards(x_vals, occupancy, perm):
+def panel_shards(x_vals, occupancy, perm):
     row_devices = lax.axis_size("row")
     panels = lax.axis_size("col")
     own_row = lax.axis_index("row")
@@ -209,6 +213,545 @@
     return spread(stepped, source, target, panel_cols)
 
 
+class Place:
+    def __init__(self, panels):
+        self.depth = panels // 2
+        self.quarter = panels // 4
+        row, col = lax.axis_index("row"), lax.axis_index("col")
+        self.half, self.core = row // 2, row % 2
+        self.level, self.lane = col // 2, col % 2
+        self.step = jnp.where(self.half == 0, self.level, self.depth - 1 - self.level)
+        self.ring = self.half * self.depth + self.step
+
+    def device(self, half, core, level, lane):
+        return (2 * half + core, 2 * level + lane)
+
+    def at_ring(self, ring):
+        half = ring // self.depth
+        step = ring % self.depth
+        level = jnp.where(half == 0, step, self.depth - 1 - step)
+        return self.device(half, self.core, level, self.lane)
+
+    def neighbour(self, by):
+        return self.at_ring((self.ring + by + 2 * self.depth) % (2 * self.depth))
+
+    def group_target(self):
+        step = self.core * self.quarter + self.level // 2
+        level = jnp.where(self.half == 0, step, self.depth - 1 - step)
+        return self.device(self.half, 1 - self.level % 2, level, self.lane)
+
+    def group_source(self):
+        level = 2 * (self.step % self.quarter) + 1 - self.core
+        return self.device(self.half, self.step // self.quarter, level, self.lane)
+
+
+def remote(source, target, send, recv, device):
+    return pltpu.make_async_remote_copy(
+        src_ref=source,
+        dst_ref=target,
+        send_sem=send,
+        recv_sem=recv,
+        device_id=device,
+        device_id_type=MESH,
+    )
+
+
+def residue_of(perm, panels, panel_cols, spot):
+    found = jnp.int32(0)
+    for n in range(panels):
+        found = found + jnp.where(perm[n] // panel_cols == spot, n, 0)
+    return found
+
+
+def relayout_kernel(
+    panels, spots, present, perm, x_ref, marks_in,
+    out_ref, marks_ref, pick_ref, sort_ref, late_ref, mid, wide,
+):
+    t = pl.program_id(0)
+    band, area = x_ref.shape[1:]
+    edge = out_ref.shape[1]
+    lanes = 2 * edge
+    pairs = area // lanes
+    pitch = mid.shape[0] // pairs
+    low = lax.broadcasted_iota(jnp.int32, (pairs, lanes), 1) < edge
+
+    @pl.when(t == 0)
+    def _():
+        marks = marks_in[...]
+        count = marks.shape[0]
+        left = jnp.concatenate([marks.astype(jnp.float32)] * count, axis=1)
+        at = (count, count * band)
+        own = lax.broadcasted_iota(jnp.int32, at, 1) // band == lax.broadcasted_iota(
+            jnp.int32, at, 0
+        )
+        to = (count * band, marks_ref.shape[1])
+        entry, lane = (lax.broadcasted_iota(jnp.int32, to, n) for n in range(2))
+        right = (lane // edge - entry // band == entry % band).astype(jnp.float32)
+        marks_ref[...] = jnp.dot(
+            jnp.where(own, left, 0.0).astype(jnp.bfloat16),
+            right.astype(jnp.bfloat16),
+            preferred_element_type=jnp.float32,
+        ).astype(marks_ref.dtype)
+        panel_cols = perm.shape[0] // panels
+        first = 4 * (lax.axis_index("row") % 2) + lax.axis_index("col") % 2
+        residues = [residue_of(perm, panels, panel_cols, first + 2 * h) for h in range(2)]
+        entry, lane = (lax.broadcasted_iota(jnp.int32, pick_ref.shape, n) for n in range(2))
+        base = jnp.where(lane < edge, residues[0] * edge, (residues[1] - 1) * edge)
+        pick_ref[...] = (entry == base + lane).astype(jnp.float32).astype(pick_ref.dtype)
+        lane = lax.broadcasted_iota(jnp.int32, (1, lanes), 1)
+        own = jnp.where(lane < edge, residues[0], residues[1])
+        to, entry = (
+            lax.broadcasted_iota(jnp.int32, (edge, sort_ref.shape[1]), n) for n in range(2)
+        )
+        for n in range(spots):
+            spot = residue_of(perm, panels, panel_cols, n)
+            sort_ref[n * edge : (n + 1) * edge, :] = (
+                (entry == to + spot * edge).astype(jnp.float32).astype(sort_ref.dtype)
+            )
+            late_ref[n : n + 1, :] = (own < spot).astype(jnp.float32)
+
+    for p in range(pairs):
+        mid[p * pitch : p * pitch + band, :] = x_ref[
+            0, :, p * lanes : (p + 1) * lanes
+        ].astype(jnp.float32)
+    for w in range(band // 2):
+        one = mid[pl.ds(2 * w, pairs, stride=pitch), :]
+        two = mid[pl.ds(2 * w + 1, pairs, stride=pitch), :]
+        one = jnp.where(present[t, 2 * w] == 1, one, 0.0)
+        two = jnp.where(present[t, 2 * w + 1] == 1, two, 0.0)
+        wide[w, pl.ds(0, pairs, stride=2), :] = jnp.where(low, one, pltpu.roll(two, edge, 1))
+        wide[w, pl.ds(1, pairs, stride=2), :] = jnp.where(low, pltpu.roll(one, edge, 1), two)
+    for w in range(band // 2):
+        out_ref[0, :, w * lanes : (w + 1) * lanes] = wide[w].astype(out_ref.dtype)
+
+
+def relayout(x_vals, occupancy, perm, panels, edge):
+    count, band, area = x_vals.shape
+    lanes = 2 * edge
+    octet = count * edge
+    return pl.pallas_call(
+        functools.partial(relayout_kernel, panels, count),
+        out_shape=(
+            jax.ShapeDtypeStruct((count, edge, band * edge), x_vals.dtype),
+            jax.ShapeDtypeStruct((count, (band + count) * edge), x_vals.dtype),
+            jax.ShapeDtypeStruct((octet, lanes), x_vals.dtype),
+            jax.ShapeDtypeStruct((octet, octet), x_vals.dtype),
+            jax.ShapeDtypeStruct((count, lanes), jnp.float32),
+        ),
+        grid_spec=pltpu.PrefetchScalarGridSpec(
+            num_scalar_prefetch=2,
+            grid=(count,),
+            in_specs=[
+                pl.BlockSpec((1, band, area), lambda t, *_: (t, 0, 0)),
+                pl.BlockSpec((count, band), lambda t, *_: (0, 0)),
+            ],
+            out_specs=(
+                pl.BlockSpec((1, edge, band * edge), lambda t, *_: (t, 0, 0)),
+                pl.BlockSpec((count, (band + count) * edge), lambda t, *_: (0, 0)),
+                pl.BlockSpec((octet, lanes), lambda t, *_: (0, 0)),
+                pl.BlockSpec((octet, octet), lambda t, *_: (0, 0)),
+                pl.BlockSpec((count, lanes), lambda t, *_: (0, 0)),
+            ),
+            scratch_shapes=[
+                pltpu.VMEM((area // lanes * (band + 8), lanes), jnp.float32),
+                pltpu.VMEM((band // 2, edge, lanes), jnp.float32),
+            ],
+        ),
+        compiler_params=pltpu.CompilerParams(dimension_semantics=("arbitrary",)),
+        name="relayout",
+    )(occupancy, perm, x_vals, occupancy)
+
+
+def core_kernel(
+    panels, scale, rows, marks, pick, sort, late, out,
+    all_rows, all_marks, left, tiles, square, kept, total, sorted_rows, packed,
+    move_sems, lane_sems, core_sems, relay_sems, halo_sems, square_sems, send, recv, local,
+):
+    place = Place(panels)
+    row, col = lax.axis_index("row"), lax.axis_index("col")
+    count, edge, band_lanes = rows.shape
+    octet = count * edge
+    groups = all_rows.shape[0]
+    wide, narrow = left.shape[-1], tiles.shape[-1]
+    width = pick.shape[1]
+    row_devices, pair = packed.shape[:2]
+    halves = packed.shape[3]
+    supers = out.shape[0]
+
+    target, source = place.group_target(), place.group_source()
+    lane_peer = place.device(place.half, place.core, place.level, 1 - place.lane)
+    core_peer = place.device(place.half, 1 - place.core, place.level, place.lane)
+    after, before = place.neighbour(1), place.neighbour(-1)
+    target_slot = 2 * (place.level % 2) + place.lane
+    own_slot = 2 * (1 - place.core) + place.lane
+    peer_slot = 2 * (1 - place.core) + 1 - place.lane
+    third_slot = 2 * place.core + place.lane
+    last_slot = 2 * place.core + 1 - place.lane
+    owner = place.level // 2
+    senders = []
+    for ring in range(supers):
+        half, step = ring // place.depth, ring % place.depth
+        level = step if half == 0 else place.depth - 1 - step
+        senders.append((2 * half + owner, 2 * level + place.lane))
+    receivers = [
+        (dest, 2 * (2 * place.core + h) + place.lane)
+        for dest in range(row_devices)
+        for h in range(pair)
+    ]
+
+    def is_here(device):
+        return jnp.logical_and(device[0] == row, device[1] == col)
+
+    barrier = pltpu.get_barrier_semaphore()
+    for device in (source, lane_peer, core_peer, after, before):
+        pl.semaphore_signal(barrier, inc=1, device_id=device, device_id_type=MESH)
+    for device in senders:
+
+        @pl.when(jnp.logical_not(is_here(device)))
+        def _(device=device):
+            pl.semaphore_signal(barrier, inc=1, device_id=device, device_id_type=MESH)
+
+    expected = 5 + len(receivers)
+    pl.semaphore_wait(barrier, jnp.where(owner == place.core, expected - 1, expected))
+
+    def copy_of(n, sems, device, slot, first=False):
+        origin = rows.at[n] if first else all_rows.at[slot, n]
+        return remote(origin, all_rows.at[slot, n], sems.at[0, n], sems.at[1, n], device)
+
+    def mark_of(sems, device, slot, first=False):
+        origin = marks if first else all_marks.at[slot]
+        return remote(
+            origin, all_marks.at[slot], sems.at[0, count], sems.at[1, count], device
+        )
+
+    mark_copies = [
+        mark_of(move_sems, target, target_slot, True),
+        mark_of(lane_sems, lane_peer, own_slot),
+        mark_of(core_sems, core_peer, own_slot),
+        mark_of(relay_sems, core_peer, peer_slot),
+    ]
+    mark_copies[0].start()
+
+    @pl.loop(0, count)
+    def _(n):
+        copy_of(n, move_sems, target, target_slot, True).start()
+
+    @pl.loop(0, groups)
+    def _(t):
+        left[t] = jnp.zeros(left.shape[1:], left.dtype)
+
+    def lay(slot, m):
+        base = pl.multiple_of(2 * m * edge, 2 * edge)
+        zeros = jnp.zeros((edge, edge), left.dtype)
+        reach = pl.ds(base, band_lanes + 2 * edge)
+        left[slot, pl.ds(base, edge), pl.ds(base, band_lanes)] = all_rows[slot, 2 * m]
+        left[slot, pl.ds(pl.multiple_of(base + edge, edge), edge), reach] = jnp.concatenate(
+            [zeros, all_rows[slot, 2 * m + 1], zeros], axis=1
+        )
+        chosen = pick[...]
+        for o in range(wide // octet):
+            tiles[slot + 2, pl.ds(base, 2 * edge), o * width : (o + 1) * width] = jnp.dot(
+                left[slot, pl.ds(base, 2 * edge), o * octet : (o + 1) * octet],
+                chosen,
+                preferred_element_type=jnp.float32,
+            ).astype(tiles.dtype)
+
+    mark_copies[0].wait_recv()
+    mark_copies[1].start()
+    mark_copies[2].start()
+
+    @pl.loop(0, count // 2)
+    def _(m):
+        for n in (2 * m, 2 * m + 1):
+            copy_of(n, move_sems, target, target_slot, True).wait_recv()
+            copy_of(n, lane_sems, lane_peer, own_slot).start()
+            copy_of(n, core_sems, core_peer, own_slot).start()
+        lay(own_slot, m)
+        for n in (2 * m, 2 * m + 1):
+            copy_of(n, lane_sems, lane_peer, own_slot).wait_recv()
+            copy_of(n, relay_sems, core_peer, peer_slot).start()
+        lay(peer_slot, m)
+        for n in (2 * m, 2 * m + 1):
+            copy_of(n, core_sems, core_peer, own_slot).wait_recv()
+        lay(third_slot, m)
+        for n in (2 * m, 2 * m + 1):
+            copy_of(n, relay_sems, core_peer, peer_slot).wait_recv()
+        lay(last_slot, m)
+
+    def halo(ref, sems):
+        step = narrow // 5
+        moves = (
+            (groups + 1, 1, slice(step, narrow), after),
+            (groups, 0, slice(2 * step, narrow), after),
+            (2, groups + 2, slice(0, 4 * step), before),
+            (3, groups + 3, slice(0, 3 * step), before),
+        )
+        return [
+            remote(
+                ref.at[origin, :, lanes], ref.at[to, :, lanes], sems.at[0, n], sems.at[1, n], device
+            )
+            for n, (origin, to, lanes, device) in enumerate(moves)
+        ]
+
+    first_halo = halo(tiles, halo_sems)
+    for copy in first_halo:
+        copy.start()
+
+    mark_copies[1].wait_recv()
+    mark_copies[3].start()
+    mark_copies[2].wait_recv()
+    mark_copies[3].wait_recv()
+    for t in range(groups):
+        for o in range(wide // octet):
+            kept[t, :, o * width : (o + 1) * width] = jnp.dot(
+                all_marks[t, :, o * octet : (o + 1) * octet],
+                pick[...],
+                preferred_element_type=jnp.float32,
+            )
+
+    def term(ref, t, by, fresh=False):
+        step = narrow // 5
+        reach = narrow - abs(by) * step
+        first = 0 if by >= 0 else narrow - reach
+        to = max(by, 0) * step
+        update = jnp.dot(
+            left[t, :, (2 + by) * octet : (3 + by) * octet],
+            ref[t + 2 + by, :, first : first + reach],
+            preferred_element_type=jnp.float32,
+        )
+        if fresh:
+            total[t] = update
+        else:
+            total[t, :, to : to + reach] += update
+
+    def own_terms(ref):
+        @pl.loop(0, groups)
+        def _(t):
+            term(ref, t, 0, True)
+            for by in (-2, -1, 1, 2):
+
+                @pl.when(jnp.logical_and(t + by >= 0, t + by < groups))
+                def _(by=by):
+                    term(ref, t, by)
+
+    def halo_terms(ref, t):
+        for by in (-2, -1, 1, 2):
+            if not 0 <= t + by < groups:
+                term(ref, t, by)
+
+    own_terms(tiles)
+    second_halo = halo(square, square_sems)
+    waits = {1: (0,), 0: (1,), 2: (2,), 3: (3,)}
+    sends = {1: 3, 0: 2, 2: 1, 3: 0}
+    for t in (1, 0, 2, 3):
+        for n in waits[t]:
+            first_halo[n].wait_recv()
+        halo_terms(tiles, t)
+        for r in range(count):
+            at = slice(r * edge, (r + 1) * edge)
+            square[t + 2, at, :] = (total[t, at, :] * kept[t, r : r + 1, :]).astype(square.dtype)
+        second_halo[{1: 3, 0: 2, 2: 1, 3: 0}[t]].start()
+
+    own_terms(square)
+    lanes = 2 * edge
+    low = lax.broadcasted_iota(jnp.int32, (edge, lanes), 1) < edge
+
+    def delivery(t, n):
+        dest, h = n // pair, n % pair
+        return remote(
+            packed.at[dest, h, t],
+            out.at[place.ring, t],
+            send.at[n, t],
+            recv.at[place.ring, t],
+            receivers[n],
+        )
+
+    def kept_here(t, n):
+        return pltpu.make_async_copy(
+            packed.at[n // pair, n % pair, t], out.at[place.ring, t], local.at[t]
+        )
+
+    def each_receiver(t, away, here):
+        for n, device in enumerate(receivers):
+
+            @pl.when(is_here(device))
+            def _(n=n):
+                here(kept_here(t, n))
+
+            @pl.when(jnp.logical_not(is_here(device)))
+            def _(n=n):
+                away(delivery(t, n))
+
+    for t in (1, 0, 2, 3):
+        for n in waits[t]:
+            second_halo[n].wait_recv()
+        halo_terms(square, t)
+        for r in range(count):
+            at = slice(r * edge, (r + 1) * edge)
+            total[t, at, :] = 1.5 * tiles[t + 2, at, :].astype(jnp.float32) - scale * (
+                total[t, at, :] * kept[t, r : r + 1, :]
+            )
+        sorted_rows[...] = jnp.dot(
+            sort[...], total[t].astype(packed.dtype), preferred_element_type=jnp.float32
+        )
+        for n in range(row_devices * halves):
+            dest, e = n // halves, n % halves
+            at = slice(n * edge, (n + 1) * edge)
+            shift = late[n : n + 1, :] > 0.5
+            parts = [sorted_rows[at, o * lanes : (o + 1) * lanes] for o in range(narrow // lanes)]
+            parts = [jnp.where(shift, two, one) for one, two in zip(parts, parts[1:])]
+            turned = [pltpu.roll(part, edge, 1) for part in parts]
+            for w in range(len(parts) // 2):
+                to = slice(w * lanes, (w + 1) * lanes)
+                packed[dest, 0, t, e, :, to] = jnp.where(
+                    low, parts[2 * w], turned[2 * w + 1]
+                ).astype(packed.dtype)
+                packed[dest, 1, t, e, :, to] = jnp.where(
+                    low, turned[2 * w], parts[2 * w + 1]
+                ).astype(packed.dtype)
+        each_receiver(t, lambda copy: copy.start(), lambda copy: copy.start())
+
+    for copy in mark_copies + first_halo + second_halo:
+        copy.wait_send()
+
+    @pl.loop(0, count)
+    def _(n):
+        copy_of(n, move_sems, target, target_slot, True).wait_send()
+        copy_of(n, lane_sems, lane_peer, own_slot).wait_send()
+        copy_of(n, core_sems, core_peer, own_slot).wait_send()
+        copy_of(n, relay_sems, core_peer, peer_slot).wait_send()
+
+    for t in (1, 0, 2, 3):
+        for n, device in enumerate(senders):
+
+            @pl.when(jnp.logical_not(is_here(device)))
+            def _(t=t, n=n, device=device):
+                remote(
+                    packed.at[0, 0, t], out.at[n, t], send.at[0, t], recv.at[n, t], device
+                ).wait_recv()
+
+        each_receiver(t, lambda copy: copy.wait_send(), lambda copy: copy.wait())
+
+
+def band_step(rows, marks, pick, sort, late, row_devices, panels, block_count, scale):
+    count, edge, band_lanes = rows.shape
+    octet, wide = count * edge, marks.shape[-1]
+    narrow = wide // octet * 2 * edge
+    halves = panels // row_devices
+    supers = block_count // (4 * count)
+    vmem = pl.BlockSpec(memory_space=pltpu.VMEM)
+    kind = rows.dtype
+    out = (supers, 4, halves, edge, 4 * edge)
+    dma = pltpu.SemaphoreType.DMA
+    return pl.pallas_call(
+        functools.partial(core_kernel, panels, scale),
+        out_shape=jax.ShapeDtypeStruct(out, kind),
+        in_specs=[ANY, ANY, vmem, vmem, vmem],
+        out_specs=ANY,
+        scratch_shapes=[
+            pltpu.VMEM((4,) + rows.shape, kind),
+            pltpu.VMEM((4,) + marks.shape, kind),
+            pltpu.VMEM((4, octet, wide), kind),
+            pltpu.VMEM((8, octet, narrow), kind),
+            pltpu.VMEM((8, octet, narrow), kind),
+            pltpu.VMEM((4, count, narrow), jnp.float32),
+            pltpu.VMEM((4, octet, narrow), jnp.float32),
+            pltpu.VMEM((octet, narrow), jnp.float32),
+            pltpu.VMEM((row_devices, 2) + out[1:], kind),
+            dma((2, count + 1)),
+            dma((2, count + 1)),
+            dma((2, count + 1)),
+            dma((2, count + 1)),
+            dma((2, 4)),
+            dma((2, 4)),
+            dma((2 * row_devices, 4)),
+            dma((supers, 4)),
+            dma((4,)),
+        ],
+        compiler_params=pltpu.CompilerParams(
+            collective_id=0, has_side_effects=True, vmem_limit_bytes=60 * 2**20
+        ),
+        name="band_step",
+    )(rows, marks, pick, sort, late)
+
+
+def place_kernel(panels, perm, parts_ref, out_ref, origins):
+    supers, groups, halves, edge, width = parts_ref.shape
+    count = supers * groups
+    lanes = 2 * edge
+    rows = out_ref.shape[0] // edge
+    half = lax.broadcasted_iota(jnp.int32, (edge, lanes), 1) // edge
+    first = pl.program_id(0) * rows
+    e = first // count
+
+    @pl.when(first == 0)
+    def _():
+        @pl.loop(0, count)
+        def _(n):
+            origins[perm[n * panels] % count] = n
+
+    residue = residue_of(perm, panels, count, lax.axis_index("col"))
+    spot = residue_of(perm, panels, count, lax.axis_index("row") * halves + e)
+    late = (residue < spot).astype(jnp.int32)
+    out_ref[...] = jnp.zeros_like(out_ref)
+
+    @pl.loop(0, rows)
+    def _(n):
+        origin = origins[lax.rem(first + n, count)]
+        at = pl.ds(pl.multiple_of(n * edge, edge), edge)
+        base = origin - 2 + late + count
+        for w in range(width // lanes):
+            tile = parts_ref[
+                origin // groups, lax.rem(origin, groups), e, :, w * lanes : (w + 1) * lanes
+            ].astype(jnp.float32)
+            rolled = pltpu.roll(tile, edge, 1)
+            for side in range(2):
+                block = perm[lax.rem(base + 2 * w + side, count) * panels] % count
+                odd = lax.rem(block, 2)
+                value = jnp.where(odd == side, tile, rolled)
+                value = jnp.where(half == odd, value, 0.0).astype(out_ref.dtype)
+                to = pl.ds(pl.multiple_of((block // 2) * lanes, lanes), lanes)
+                out_ref[at, to] += value
+
+
+def place_blocks(parts, perm, panels):
+    supers, groups, halves, edge, width = parts.shape
+    count = supers * groups
+    rows = min(count, 8)
+    return pl.pallas_call(
+        functools.partial(place_kernel, panels),
+        out_shape=jax.ShapeDtypeStruct((halves * count * edge, count * edge), parts.dtype),
+        grid_spec=pltpu.PrefetchScalarGridSpec(
+            num_scalar_prefetch=1,
+            grid=(halves * count // rows,),
+            in_specs=[pl.BlockSpec(parts.shape, lambda g, *_: (0, 0, 0, 0, 0))],
+            out_specs=pl.BlockSpec((rows * edge, count * edge), lambda g, *_: (g, 0)),
+            scratch_shapes=[pltpu.SMEM((count,), jnp.int32)],
+        ),
+        compiler_params=pltpu.CompilerParams(dimension_semantics=("arbitrary",)),
+        name="place_blocks",
+    )(perm, parts)
+
+
+def band_shards(x_vals, occupancy, perm):
+    row_devices = lax.axis_size("row")
+    panels = lax.axis_size("col")
+    band = x_vals.shape[1]
+    made = relayout(x_vals, occupancy, perm, panels, BLOCK_EDGE)
+    scale = 0.5 / (BLOCK_EDGE * band)
+    parts = band_step(*made, row_devices, panels, perm.shape[0], scale)
+    return place_blocks(parts, perm, panels)
+
+
+def shards(x_vals, occupancy, perm):
+    row_devices = lax.axis_size("row")
+    panels = lax.axis_size("col")
+    count, band, _ = x_vals.shape
+    if row_devices == 4 and panels == count == 2 * row_devices and band == 4 * count:
+        return band_shards(x_vals, occupancy, perm)
+    return panel_shards(x_vals, occupancy, perm)
+
+
 def solution(mesh):
     return jax.shard_map(
         shards,

time: 677 us -> 205 us (0.30); the launches traced: 668 us -> 204 us
  waiting for transfers between devices: 253 us -> 0 us
  blocking collectives: 117 us -> 0 us
  other arithmetic: 83.2 us -> 0 us
  Pallas kernels: 162 us -> 204 us
  local copies, waits for them, and re-layouts: 33.6 us -> 0 us
  between operations: 17 us -> 0.01 us
    all_gather x3 -> x0, waiting for transfers between devices: 253 us -> none  [the longest x1 147 us: shards(): left = lax.all_gather(tile[None], 'col', axis=0, tiled=True)]
    all_gather x1 -> x0, blocking collectives: 64.3 us -> none  [shards(): lax.all_gather(kept.reshape(local_rows, panels * slots), ('row', 'col'),...]
    all_to_all x1 -> x0, blocking collectives: 52.8 us -> none  [shards(): lax.all_to_all(values, 'col', split_axis=0, concat_axis=0, tiled=True)]
    pallas_call x3, Pallas kernels: 162 us -> 204 us  [the longest x1 184 us: band_step(): pl.pallas_call(functools.partial(core_kernel, panels, scale), out_shape=j...]
    concatenate x3 -> x0, other arithmetic: 36.2 us -> none  [widen(): jnp.concatenate([jnp.where(high, zero, values), jnp.where(high, values, z...]
    select_n x7 -> x0, other arithmetic: 28.3 us -> none  [the longest x3 27.3 us: widen(): jnp.where(high, zero, values)]
    reshape x6 -> x0, local copies, waits for them, and re-layouts: 26.4 us -> none  [the longest x2 19.3 us: shards(): values.reshape(panels, local_rows, slots, BLOCK_EDGE, BLOCK_EDGE)]
    convert_element_type x6 -> x0, other arithmetic: 14 us -> none  [the longest x1 6.41 us: shards(): narrow(banded_product(left_wide, far_wide, order, False, slots))]
  transfers between devices with their start and end apart: 3 -> 0, of which waited for: 3 -> 0; matrix products, arithmetic and copies ran while one was open for 3% -> 0% of each run, Pallas kernels for 0% -> 0%
where the time goes in v2:
time: 205 us; the launch traced here: 204 us
  Pallas kernels  204 us (100%)
    pallas_call x1, Pallas kernels, band_step(): pl.pallas_call(functools.partial(core_kernel, panels, scale), out_shape=j...  184 us
    pallas_call x1, Pallas kernels, place_blocks(): pl.pallas_call(functools.partial(place_kernel, panels), out_shape=jax.Sha...  12.8 us
    pallas_call x1, Pallas kernels, relayout(): pl.pallas_call(functools.partial(relayout_kernel, panels, count), out_sha...  7.83 us

profile of v2, /device:TPU:3, one launch (start us, length us, event | category | flops | bytes accessed | tf_op | source)
XLA Modules:
  0.0 204.2 jit_solution(6333340779987822620)
XLA Ops:
  0.0 7.8 %relayout.1 = (bf16[8,64,2048]{2,1,0:T(8,128)(2,1)}, bf16[8,2560]{1,0:T(8,128)(2,1)}, bf16[512,128]{1,0:T(8,128)(2,1)}, bf16[512,512]{1,0:T(8,128)(2,1)}, f32[8,128]{1,0:T(8,128)}) custom-call(s32[8,32]{1,0:T(8,128)} %marks_in.1, s32[256]{0:T(256)} %perm.3, bf16[8,32,4096]{2,1,0:T(8,128)(2,1)} %x_ref.1, s32[8,32]{1,0:T(8,128)} %marks_in.1), custom_call_target="tpu_custom_call" | custom-call | tf_op jit(solution)/shard_map/relayout/pallas_call | solution.py:332
  7.8 183.6 %band_step.1.parts_ref = bf16[8,4,2,64,256]{4,3,2,1,0:T(8,128)(2,1)} custom-call(bf16[8,64,2048]{2,1,0:T(8,128)(2,1)} %get-tuple-element.10.rows, bf16[8,2560]{1,0:T(8,128)(2,1)} %get-tuple-element.11.marks, bf16[512,128]{1,0:T(8,128)(2,1)} %get-tuple-element.12.pick, bf16[512,512]{1,0:T(8,128)(2,1)} %get-tuple-element.13.sort, f32[8,128]{1,0:T(8,128)} %get-tuple-element.14.late), custom_call_target="tpu_custom_call" | custom-call | tf_op jit(solution)/shard_map/band_step/pallas_call | solution.py:646
  191.4 12.8 %place_blocks.1 = bf16[4096,2048]{1,0:T(8,128)(2,1)} custom-call(s32[256]{0:T(256)} %perm.3, bf16[8,4,2,64,256]{4,3,2,1,0:T(8,128)(2,1)} %band_step.1.parts_ref), custom_call_target="tpu_custom_call" | custom-call | tf_op jit(solution)/shard_map/place_blocks/pallas_call | solution.py:721

commit v3 on v2

--- a/solution.py
+++ b/solution.py
@@ -263,107 +263,9 @@
     return found
 
 
-def relayout_kernel(
-    panels, spots, present, perm, x_ref, marks_in,
-    out_ref, marks_ref, pick_ref, sort_ref, late_ref, mid, wide,
-):
-    t = pl.program_id(0)
-    band, area = x_ref.shape[1:]
-    edge = out_ref.shape[1]
-    lanes = 2 * edge
-    pairs = area // lanes
-    pitch = mid.shape[0] // pairs
-    low = lax.broadcasted_iota(jnp.int32, (pairs, lanes), 1) < edge
-
-    @pl.when(t == 0)
-    def _():
-        marks = marks_in[...]
-        count = marks.shape[0]
-        left = jnp.concatenate([marks.astype(jnp.float32)] * count, axis=1)
-        at = (count, count * band)
-        own = lax.broadcasted_iota(jnp.int32, at, 1) // band == lax.broadcasted_iota(
-            jnp.int32, at, 0
-        )
-        to = (count * band, marks_ref.shape[1])
-        entry, lane = (lax.broadcasted_iota(jnp.int32, to, n) for n in range(2))
-        right = (lane // edge - entry // band == entry % band).astype(jnp.float32)
-        marks_ref[...] = jnp.dot(
-            jnp.where(own, left, 0.0).astype(jnp.bfloat16),
-            right.astype(jnp.bfloat16),
-            preferred_element_type=jnp.float32,
-        ).astype(marks_ref.dtype)
-        panel_cols = perm.shape[0] // panels
-        first = 4 * (lax.axis_index("row") % 2) + lax.axis_index("col") % 2
-        residues = [residue_of(perm, panels, panel_cols, first + 2 * h) for h in range(2)]
-        entry, lane = (lax.broadcasted_iota(jnp.int32, pick_ref.shape, n) for n in range(2))
-        base = jnp.where(lane < edge, residues[0] * edge, (residues[1] - 1) * edge)
-        pick_ref[...] = (entry == base + lane).astype(jnp.float32).astype(pick_ref.dtype)
-        lane = lax.broadcasted_iota(jnp.int32, (1, lanes), 1)
-        own = jnp.where(lane < edge, residues[0], residues[1])
-        to, entry = (
-            lax.broadcasted_iota(jnp.int32, (edge, sort_ref.shape[1]), n) for n in range(2)
-        )
-        for n in range(spots):
-            spot = residue_of(perm, panels, panel_cols, n)
-            sort_ref[n * edge : (n + 1) * edge, :] = (
-                (entry == to + spot * edge).astype(jnp.float32).astype(sort_ref.dtype)
-            )
-            late_ref[n : n + 1, :] = (own < spot).astype(jnp.float32)
-
-    for p in range(pairs):
-        mid[p * pitch : p * pitch + band, :] = x_ref[
-            0, :, p * lanes : (p + 1) * lanes
-        ].astype(jnp.float32)
-    for w in range(band // 2):
-        one = mid[pl.ds(2 * w, pairs, stride=pitch), :]
-        two = mid[pl.ds(2 * w + 1, pairs, stride=pitch), :]
-        one = jnp.where(present[t, 2 * w] == 1, one, 0.0)
-        two = jnp.where(present[t, 2 * w + 1] == 1, two, 0.0)
-        wide[w, pl.ds(0, pairs, stride=2), :] = jnp.where(low, one, pltpu.roll(two, edge, 1))
-        wide[w, pl.ds(1, pairs, stride=2), :] = jnp.where(low, pltpu.roll(one, edge, 1), two)
-    for w in range(band // 2):
-        out_ref[0, :, w * lanes : (w + 1) * lanes] = wide[w].astype(out_ref.dtype)
-
-
-def relayout(x_vals, occupancy, perm, panels, edge):
-    count, band, area = x_vals.shape
-    lanes = 2 * edge
-    octet = count * edge
-    return pl.pallas_call(
-        functools.partial(relayout_kernel, panels, count),
-        out_shape=(
-            jax.ShapeDtypeStruct((count, edge, band * edge), x_vals.dtype),
-            jax.ShapeDtypeStruct((count, (band + count) * edge), x_vals.dtype),
-            jax.ShapeDtypeStruct((octet, lanes), x_vals.dtype),
-            jax.ShapeDtypeStruct((octet, octet), x_vals.dtype),
-            jax.ShapeDtypeStruct((count, lanes), jnp.float32),
-        ),
-        grid_spec=pltpu.PrefetchScalarGridSpec(
-            num_scalar_prefetch=2,
-            grid=(count,),
-            in_specs=[
-                pl.BlockSpec((1, band, area), lambda t, *_: (t, 0, 0)),
-                pl.BlockSpec((count, band), lambda t, *_: (0, 0)),
-            ],
-            out_specs=(
-                pl.BlockSpec((1, edge, band * edge), lambda t, *_: (t, 0, 0)),
-                pl.BlockSpec((count, (band + count) * edge), lambda t, *_: (0, 0)),
-                pl.BlockSpec((octet, lanes), lambda t, *_: (0, 0)),
-                pl.BlockSpec((octet, octet), lambda t, *_: (0, 0)),
-                pl.BlockSpec((count, lanes), lambda t, *_: (0, 0)),
-            ),
-            scratch_shapes=[
-                pltpu.VMEM((area // lanes * (band + 8), lanes), jnp.float32),
-                pltpu.VMEM((band // 2, edge, lanes), jnp.float32),
-            ],
-        ),
-        compiler_params=pltpu.CompilerParams(dimension_semantics=("arbitrary",)),
-        name="relayout",
-    )(occupancy, perm, x_vals, occupancy)
-
-
 def core_kernel(
-    panels, scale, rows, marks, pick, sort, late, out,
+    panels, scale, present, perm, x_ref, flags, out,
+    rows, marks, pick, sort, late, mid, pairs,
     all_rows, all_marks, left, tiles, square, kept, total, sorted_rows, packed,
     move_sems, lane_sems, core_sems, relay_sems, halo_sems, square_sems, send, recv, local,
 ):
@@ -414,14 +316,18 @@
     expected = 5 + len(receivers)
     pl.semaphore_wait(barrier, jnp.where(owner == place.core, expected - 1, expected))
 
+    def piece_of(ref, n):
+        return ref.at[n // 2, pl.ds(n % 2 * (edge // 2), edge // 2)]
+
     def copy_of(n, sems, device, slot, first=False):
-        origin = rows.at[n] if first else all_rows.at[slot, n]
-        return remote(origin, all_rows.at[slot, n], sems.at[0, n], sems.at[1, n], device)
+        landing = piece_of(all_rows.at[slot], n)
+        origin = piece_of(rows, n) if first else landing
+        return remote(origin, landing, sems.at[0, n], sems.at[1, n], device)
 
     def mark_of(sems, device, slot, first=False):
         origin = marks if first else all_marks.at[slot]
         return remote(
-            origin, all_marks.at[slot], sems.at[0, count], sems.at[1, count], device
+            origin, all_marks.at[slot], sems.at[0, 2 * count], sems.at[1, 2 * count], device
         )
 
     mark_copies = [
@@ -430,11 +336,70 @@
         mark_of(core_sems, core_peer, own_slot),
         mark_of(relay_sems, core_peer, peer_slot),
     ]
+    lanes = 2 * edge
+    low = lax.broadcasted_iota(jnp.int32, (edge, lanes), 1) < edge
+    panel_cols = perm.shape[0] // panels
+    band, area = x_ref.shape[1:]
+    tall = area // lanes
+    pitch = mid.shape[0] // tall
+
+    def relay_row(t):
+        for p in range(tall):
+            mid[p * pitch : p * pitch + band, :] = x_ref[
+                t, :, p * lanes : (p + 1) * lanes
+            ].astype(jnp.float32)
+        for w in range(band // 2):
+            one = mid[pl.ds(2 * w, tall, stride=pitch), :] * present[t, 2 * w].astype(jnp.float32)
+            two = mid[pl.ds(2 * w + 1, tall, stride=pitch), :] * present[t, 2 * w + 1].astype(
+                jnp.float32
+            )
+            lower = low[:tall]
+            pairs[w, pl.ds(0, tall, stride=2), :] = jnp.where(
+                lower, one, pltpu.roll(two, edge, 1)
+            )
+            pairs[w, pl.ds(1, tall, stride=2), :] = jnp.where(
+                lower, pltpu.roll(one, edge, 1), two
+            )
+        for w in range(band // 2):
+            rows[t, :, w * lanes : (w + 1) * lanes] = pairs[w].astype(rows.dtype)
+
+    @pl.loop(0, count)
+    def _(t):
+        relay_row(t)
+
+        @pl.when(t > 0)
+        def _():
+            for n in range(2):
+                copy_of(2 * (t - 1) + n, move_sems, target, target_slot, True).start()
+
+    wide_flags = jnp.concatenate([flags[...].astype(jnp.float32)] * count, axis=1)
+    at = (count, count * band)
+    own = lax.broadcasted_iota(jnp.int32, at, 1) // band == lax.broadcasted_iota(jnp.int32, at, 0)
+    to = (count * band, wide)
+    entry, lane = (lax.broadcasted_iota(jnp.int32, to, n) for n in range(2))
+    spread = (lane // edge - entry // band == entry % band).astype(jnp.float32)
+    marks[...] = jnp.dot(
+        jnp.where(own, wide_flags, 0.0).astype(marks.dtype),
+        spread.astype(marks.dtype),
+        preferred_element_type=jnp.float32,
+    ).astype(marks.dtype)
+    for n in range(2):
+        copy_of(2 * (count - 1) + n, move_sems, target, target_slot, True).start()
+    first = 4 * place.core + place.lane
+    residues = [residue_of(perm, panels, panel_cols, first + 2 * h) for h in range(2)]
+    entry, lane = (lax.broadcasted_iota(jnp.int32, pick.shape, n) for n in range(2))
+    base = jnp.where(lane < edge, residues[0] * edge, (residues[1] - 1) * edge)
+    pick[...] = (entry == base + lane).astype(jnp.float32).astype(pick.dtype)
     mark_copies[0].start()
-
-    @pl.loop(0, count)
-    def _(n):
-        copy_of(n, move_sems, target, target_slot, True).start()
+    lane = lax.broadcasted_iota(jnp.int32, (1, lanes), 1)
+    own = jnp.where(lane < edge, residues[0], residues[1])
+    to, entry = (lax.broadcasted_iota(jnp.int32, (edge, octet), n) for n in range(2))
+    for n in range(row_devices * halves):
+        spot = residue_of(perm, panels, panel_cols, n)
+        sort[n * edge : (n + 1) * edge, :] = (
+            (entry == to + spot * edge).astype(jnp.float32).astype(sort.dtype)
+        )
+        late[n : n + 1, :] = (own < spot).astype(jnp.float32)
 
     @pl.loop(0, groups)
     def _(t):
@@ -456,27 +421,45 @@
                 preferred_element_type=jnp.float32,
             ).astype(tiles.dtype)
 
+    rounds = count // 2
+
+    @pl.loop(0, rounds + 2)
+    def _(m):
+        @pl.when(m < rounds)
+        def _():
+            for i in range(4):
+                n = 4 * m + i
+                copy_of(n, move_sems, target, target_slot, True).wait_recv()
+                copy_of(n, lane_sems, lane_peer, own_slot).start()
+                copy_of(n, core_sems, core_peer, own_slot).start()
+
+        @pl.when(jnp.logical_and(m > 0, m <= rounds))
+        def _():
+            for i in range(4):
+                n = 4 * (m - 1) + i
+                copy_of(n, lane_sems, lane_peer, own_slot).wait_recv()
+                copy_of(n, relay_sems, core_peer, peer_slot).start()
+
+        @pl.when(m < rounds)
+        def _():
+            lay(own_slot, m)
+
+        @pl.when(jnp.logical_and(m > 0, m <= rounds))
+        def _():
+            for i in range(4):
+                copy_of(4 * (m - 1) + i, core_sems, core_peer, own_slot).wait_recv()
+            lay(peer_slot, m - 1)
+            lay(third_slot, m - 1)
+
+        @pl.when(m > 1)
+        def _():
+            for i in range(4):
+                copy_of(4 * (m - 2) + i, relay_sems, core_peer, peer_slot).wait_recv()
+            lay(last_slot, m - 2)
+
     mark_copies[0].wait_recv()
     mark_copies[1].start()
     mark_copies[2].start()
-
-    @pl.loop(0, count // 2)
-    def _(m):
-        for n in (2 * m, 2 * m + 1):
-            copy_of(n, move_sems, target, target_slot, True).wait_recv()
-            copy_of(n, lane_sems, lane_peer, own_slot).start()
-            copy_of(n, core_sems, core_peer, own_slot).start()
-        lay(own_slot, m)
-        for n in (2 * m, 2 * m + 1):
-            copy_of(n, lane_sems, lane_peer, own_slot).wait_recv()
-            copy_of(n, relay_sems, core_peer, peer_slot).start()
-        lay(peer_slot, m)
-        for n in (2 * m, 2 * m + 1):
-            copy_of(n, core_sems, core_peer, own_slot).wait_recv()
-        lay(third_slot, m)
-        for n in (2 * m, 2 * m + 1):
-            copy_of(n, relay_sems, core_peer, peer_slot).wait_recv()
-        lay(last_slot, m)
 
     def halo(ref, sems):
         step = narrow // 5
@@ -553,9 +536,6 @@
         second_halo[{1: 3, 0: 2, 2: 1, 3: 0}[t]].start()
 
     own_terms(square)
-    lanes = 2 * edge
-    low = lax.broadcasted_iota(jnp.int32, (edge, lanes), 1) < edge
-
     def delivery(t, n):
         dest, h = n // pair, n % pair
         return remote(
@@ -614,7 +594,7 @@
     for copy in mark_copies + first_halo + second_halo:
         copy.wait_send()
 
-    @pl.loop(0, count)
+    @pl.loop(0, 2 * count)
     def _(n):
         copy_of(n, move_sems, target, target_slot, True).wait_send()
         copy_of(n, lane_sems, lane_peer, own_slot).wait_send()
@@ -633,24 +613,35 @@
         each_receiver(t, lambda copy: copy.wait_send(), lambda copy: copy.wait())
 
 
-def band_step(rows, marks, pick, sort, late, row_devices, panels, block_count, scale):
-    count, edge, band_lanes = rows.shape
-    octet, wide = count * edge, marks.shape[-1]
-    narrow = wide // octet * 2 * edge
+def band_step(x_vals, occupancy, perm, row_devices, panels, scale):
+    count, band, area = x_vals.shape
+    edge = BLOCK_EDGE
+    lanes = 2 * edge
+    octet, wide = count * edge, (band + count) * edge
+    narrow = wide // octet * lanes
     halves = panels // row_devices
-    supers = block_count // (4 * count)
-    vmem = pl.BlockSpec(memory_space=pltpu.VMEM)
-    kind = rows.dtype
+    supers = perm.shape[0] // (4 * count)
+    kind = x_vals.dtype
+    rows = (count, edge, band * edge)
     out = (supers, 4, halves, edge, 4 * edge)
     dma = pltpu.SemaphoreType.DMA
+    vmem = pl.BlockSpec(memory_space=pltpu.VMEM)
+    smem = pl.BlockSpec(memory_space=pltpu.SMEM)
     return pl.pallas_call(
         functools.partial(core_kernel, panels, scale),
         out_shape=jax.ShapeDtypeStruct(out, kind),
-        in_specs=[ANY, ANY, vmem, vmem, vmem],
+        in_specs=[smem, smem, vmem, vmem],
         out_specs=ANY,
         scratch_shapes=[
-            pltpu.VMEM((4,) + rows.shape, kind),
-            pltpu.VMEM((4,) + marks.shape, kind),
+            pltpu.VMEM(rows, kind),
+            pltpu.VMEM((count, wide), kind),
+            pltpu.VMEM((octet, lanes), kind),
+            pltpu.VMEM((octet, octet), kind),
+            pltpu.VMEM((count, lanes), jnp.float32),
+            pltpu.VMEM((area // lanes * (band + 8), lanes), jnp.float32),
+            pltpu.VMEM((band // 2, edge, lanes), jnp.float32),
+            pltpu.VMEM((4,) + rows, kind),
+            pltpu.VMEM((4, count, wide), kind),
             pltpu.VMEM((4, octet, wide), kind),
             pltpu.VMEM((8, octet, narrow), kind),
             pltpu.VMEM((8, octet, narrow), kind),
@@ -658,10 +649,10 @@
             pltpu.VMEM((4, octet, narrow), jnp.float32),
             pltpu.VMEM((octet, narrow), jnp.float32),
             pltpu.VMEM((row_devices, 2) + out[1:], kind),
-            dma((2, count + 1)),
-            dma((2, count + 1)),
-            dma((2, count + 1)),
-            dma((2, count + 1)),
+            dma((2, 2 * count + 1)),
+            dma((2, 2 * count + 1)),
+            dma((2, 2 * count + 1)),
+            dma((2, 2 * count + 1)),
             dma((2, 4)),
             dma((2, 4)),
             dma((2 * row_devices, 4)),
@@ -672,7 +663,7 @@
             collective_id=0, has_side_effects=True, vmem_limit_bytes=60 * 2**20
         ),
         name="band_step",
-    )(rows, marks, pick, sort, late)
+    )(occupancy, perm, x_vals, occupancy)
 
 
 def place_kernel(panels, perm, parts_ref, out_ref, origins):
@@ -700,6 +691,7 @@
         origin = origins[lax.rem(first + n, count)]
         at = pl.ds(pl.multiple_of(n * edge, edge), edge)
         base = origin - 2 + late + count
+        made = []
         for w in range(width // lanes):
             tile = parts_ref[
                 origin // groups, lax.rem(origin, groups), e, :, w * lanes : (w + 1) * lanes
@@ -710,8 +702,9 @@
                 odd = lax.rem(block, 2)
                 value = jnp.where(odd == side, tile, rolled)
                 value = jnp.where(half == odd, value, 0.0).astype(out_ref.dtype)
-                to = pl.ds(pl.multiple_of((block // 2) * lanes, lanes), lanes)
-                out_ref[at, to] += value
+                made.append((pl.ds(pl.multiple_of((block // 2) * lanes, lanes), lanes), value))
+        for to, value in made:
+            out_ref[at, to] += value
 
 
 def place_blocks(parts, perm, panels):
@@ -737,9 +730,8 @@
     row_devices = lax.axis_size("row")
     panels = lax.axis_size("col")
     band = x_vals.shape[1]
-    made = relayout(x_vals, occupancy, perm, panels, BLOCK_EDGE)
     scale = 0.5 / (BLOCK_EDGE * band)
-    parts = band_step(*made, row_devices, panels, perm.shape[0], scale)
+    parts = band_step(x_vals, occupancy, perm, row_devices, panels, scale)
     return place_blocks(parts, perm, panels)
 
 

time: 205 us -> 181 us (0.88)
  Pallas kernels: 204 us -> 181 us
    pallas_call x1, Pallas kernels: 184 us -> 168 us  [band_step(): pl.pallas_call(functools.partial(core_kernel, panels, scale), out_shape=j...]
    pallas_call x1 -> x0, Pallas kernels: 7.83 us -> none  [relayout(): pl.pallas_call(functools.partial(relayout_kernel, panels, count), out_sha...]
where the time goes in v3:
time: 181 us
  Pallas kernels  181 us (100%)
    pallas_call x1, Pallas kernels, band_step(): pl.pallas_call(functools.partial(core_kernel, panels, scale), out_shape=j...  168 us
    pallas_call x1, Pallas kernels, place_blocks(): pl.pallas_call(functools.partial(place_kernel, panels), out_shape=jax.Sha...  12.8 us

profile of v3, /device:TPU:3, one launch (start us, length us, event | category | flops | bytes accessed | tf_op | source)
XLA Modules:
  0.0 180.7 jit_solution(14314632854472624230)
XLA Ops:
  0.0 167.9 %band_step.1.parts_ref = bf16[8,4,2,64,256]{4,3,2,1,0:T(8,128)(2,1)} custom-call(s32[8,32]{1,0:T(8,128)} %flags.1, s32[256]{0:T(256)} %perm.3, bf16[8,32,4096]{2,1,0:T(8,128)(2,1)} %x_ref.1, s32[8,32]{1,0:T(8,128)} %flags.1), custom_call_target="tpu_custom_call" | custom-call | tf_op jit(solution)/shard_map/band_step/pallas_call | solution.py:630
  167.9 12.8 %place_blocks.1 = bf16[4096,2048]{1,0:T(8,128)(2,1)} custom-call(s32[256]{0:T(256)} %perm.3, bf16[8,4,2,64,256]{4,3,2,1,0:T(8,128)(2,1)} %band_step.1.parts_ref), custom_call_target="tpu_custom_call" | custom-call | tf_op jit(solution)/shard_map/place_blocks/pallas_call | solution.py:714

commit v4 on v3

--- a/solution.py
+++ b/solution.py
@@ -264,10 +264,10 @@
 
 
 def core_kernel(
-    panels, scale, present, perm, x_ref, flags, out,
-    rows, marks, pick, sort, late, mid, pairs,
+    panels, scale, present, perm, x_vals, flags, out,
+    x_ref, rows, marks, pick, sort, late, mid, pairs,
     all_rows, all_marks, left, tiles, square, kept, total, sorted_rows, packed,
-    move_sems, lane_sems, core_sems, relay_sems, halo_sems, square_sems, send, recv, local,
+    move_sems, lane_sems, core_sems, relay_sems, halo_sems, square_sems, send, recv, local, load_sems,
 ):
     place = Place(panels)
     row, col = lax.axis_index("row"), lax.axis_index("col")
@@ -304,6 +304,13 @@
     def is_here(device):
         return jnp.logical_and(device[0] == row, device[1] == col)
 
+    def load_of(t):
+        return pltpu.make_async_copy(x_vals.at[t], x_ref.at[t], load_sems.at[t])
+
+    @pl.loop(0, count)
+    def _(t):
+        load_of(t).start()
+
     barrier = pltpu.get_barrier_semaphore()
     for device in (source, lane_peer, core_peer, after, before):
         pl.semaphore_signal(barrier, inc=1, device_id=device, device_id_type=MESH)
@@ -312,9 +319,6 @@
         @pl.when(jnp.logical_not(is_here(device)))
         def _(device=device):
             pl.semaphore_signal(barrier, inc=1, device_id=device, device_id_type=MESH)
-
-    expected = 5 + len(receivers)
-    pl.semaphore_wait(barrier, jnp.where(owner == place.core, expected - 1, expected))
 
     def piece_of(ref, n):
         return ref.at[n // 2, pl.ds(n % 2 * (edge // 2), edge // 2)]
@@ -363,15 +367,6 @@
         for w in range(band // 2):
             rows[t, :, w * lanes : (w + 1) * lanes] = pairs[w].astype(rows.dtype)
 
-    @pl.loop(0, count)
-    def _(t):
-        relay_row(t)
-
-        @pl.when(t > 0)
-        def _():
-            for n in range(2):
-                copy_of(2 * (t - 1) + n, move_sems, target, target_slot, True).start()
-
     wide_flags = jnp.concatenate([flags[...].astype(jnp.float32)] * count, axis=1)
     at = (count, count * band)
     own = lax.broadcasted_iota(jnp.int32, at, 1) // band == lax.broadcasted_iota(jnp.int32, at, 0)
@@ -383,14 +378,11 @@
         spread.astype(marks.dtype),
         preferred_element_type=jnp.float32,
     ).astype(marks.dtype)
-    for n in range(2):
-        copy_of(2 * (count - 1) + n, move_sems, target, target_slot, True).start()
     first = 4 * place.core + place.lane
     residues = [residue_of(perm, panels, panel_cols, first + 2 * h) for h in range(2)]
     entry, lane = (lax.broadcasted_iota(jnp.int32, pick.shape, n) for n in range(2))
     base = jnp.where(lane < edge, residues[0] * edge, (residues[1] - 1) * edge)
     pick[...] = (entry == base + lane).astype(jnp.float32).astype(pick.dtype)
-    mark_copies[0].start()
     lane = lax.broadcasted_iota(jnp.int32, (1, lanes), 1)
     own = jnp.where(lane < edge, residues[0], residues[1])
     to, entry = (lax.broadcasted_iota(jnp.int32, (edge, octet), n) for n in range(2))
@@ -401,6 +393,23 @@
         )
         late[n : n + 1, :] = (own < spot).astype(jnp.float32)
 
+    expected = 5 + len(receivers)
+    pl.semaphore_wait(barrier, jnp.where(owner == place.core, expected - 1, expected))
+
+    mark_copies[0].start()
+
+    @pl.loop(0, count + 1)
+    def _(t):
+        @pl.when(t < count)
+        def _():
+            load_of(t).wait()
+            relay_row(t)
+
+        @pl.when(t > 0)
+        def _():
+            for n in range(2):
+                copy_of(2 * (t - 1) + n, move_sems, target, target_slot, True).start()
+
     @pl.loop(0, groups)
     def _(t):
         left[t] = jnp.zeros(left.shape[1:], left.dtype)
@@ -421,46 +430,6 @@
                 preferred_element_type=jnp.float32,
             ).astype(tiles.dtype)
 
-    rounds = count // 2
-
-    @pl.loop(0, rounds + 2)
-    def _(m):
-        @pl.when(m < rounds)
-        def _():
-            for i in range(4):
-                n = 4 * m + i
-                copy_of(n, move_sems, target, target_slot, True).wait_recv()
-                copy_of(n, lane_sems, lane_peer, own_slot).start()
-                copy_of(n, core_sems, core_peer, own_slot).start()
-
-        @pl.when(jnp.logical_and(m > 0, m <= rounds))
-        def _():
-            for i in range(4):
-                n = 4 * (m - 1) + i
-                copy_of(n, lane_sems, lane_peer, own_slot).wait_recv()
-                copy_of(n, relay_sems, core_peer, peer_slot).start()
-
-        @pl.when(m < rounds)
-        def _():
-            lay(own_slot, m)
-
-        @pl.when(jnp.logical_and(m > 0, m <= rounds))
-        def _():
-            for i in range(4):
-                copy_of(4 * (m - 1) + i, core_sems, core_peer, own_slot).wait_recv()
-            lay(peer_slot, m - 1)
-            lay(third_slot, m - 1)
-
-        @pl.when(m > 1)
-        def _():
-            for i in range(4):
-                copy_of(4 * (m - 2) + i, relay_sems, core_peer, peer_slot).wait_recv()
-            lay(last_slot, m - 2)
-
-    mark_copies[0].wait_recv()
-    mark_copies[1].start()
-    mark_copies[2].start()
-
     def halo(ref, sems):
         step = narrow // 5
         moves = (
@@ -477,11 +446,54 @@
         ]
 
     first_halo = halo(tiles, halo_sems)
-    for copy in first_halo:
-        copy.start()
-
+    sends = {1: 3, 0: 2, 2: 1, 3: 0}
+
+    def send_tile(slot):
+        for t in range(groups):
+
+            @pl.when(slot == t)
+            def _(t=t):
+                first_halo[sends[t]].start()
+
+    rounds = count // 2
+    mark_copies[0].wait_recv()
+    mark_copies[1].start()
+    mark_copies[2].start()
+
+    @pl.loop(0, rounds)
+    def _(m):
+        for i in range(4):
+            n = 4 * m + i
+            copy_of(n, move_sems, target, target_slot, True).wait_recv()
+            copy_of(n, lane_sems, lane_peer, own_slot).start()
+            copy_of(n, core_sems, core_peer, own_slot).start()
+        lay(own_slot, m)
+
+    send_tile(own_slot)
     mark_copies[1].wait_recv()
     mark_copies[3].start()
+
+    @pl.loop(0, rounds)
+    def _(m):
+        for i in range(4):
+            n = 4 * m + i
+            copy_of(n, lane_sems, lane_peer, own_slot).wait_recv()
+            copy_of(n, relay_sems, core_peer, peer_slot).start()
+        for i in range(4):
+            copy_of(4 * m + i, core_sems, core_peer, own_slot).wait_recv()
+        lay(peer_slot, m)
+        lay(third_slot, m)
+
+    send_tile(peer_slot)
+    send_tile(third_slot)
+    @pl.loop(0, rounds)
+    def _(m):
+        for i in range(4):
+            copy_of(4 * m + i, relay_sems, core_peer, peer_slot).wait_recv()
+        lay(last_slot, m)
+
+    send_tile(last_slot)
+
     mark_copies[2].wait_recv()
     mark_copies[3].wait_recv()
     for t in range(groups):
@@ -524,16 +536,16 @@
 
     own_terms(tiles)
     second_halo = halo(square, square_sems)
+    turns = (1, 2, 0, 3)
     waits = {1: (0,), 0: (1,), 2: (2,), 3: (3,)}
-    sends = {1: 3, 0: 2, 2: 1, 3: 0}
-    for t in (1, 0, 2, 3):
+    for t in turns:
         for n in waits[t]:
             first_halo[n].wait_recv()
         halo_terms(tiles, t)
         for r in range(count):
             at = slice(r * edge, (r + 1) * edge)
             square[t + 2, at, :] = (total[t, at, :] * kept[t, r : r + 1, :]).astype(square.dtype)
-        second_halo[{1: 3, 0: 2, 2: 1, 3: 0}[t]].start()
+        second_halo[sends[t]].start()
 
     own_terms(square)
     def delivery(t, n):
@@ -562,7 +574,7 @@
             def _(n=n):
                 away(delivery(t, n))
 
-    for t in (1, 0, 2, 3):
+    for t in turns:
         for n in waits[t]:
             second_halo[n].wait_recv()
         halo_terms(square, t)
@@ -601,7 +613,7 @@
         copy_of(n, core_sems, core_peer, own_slot).wait_send()
         copy_of(n, relay_sems, core_peer, peer_slot).wait_send()
 
-    for t in (1, 0, 2, 3):
+    for t in turns:
         for n, device in enumerate(senders):
 
             @pl.when(jnp.logical_not(is_here(device)))
@@ -630,9 +642,10 @@
     return pl.pallas_call(
         functools.partial(core_kernel, panels, scale),
         out_shape=jax.ShapeDtypeStruct(out, kind),
-        in_specs=[smem, smem, vmem, vmem],
+        in_specs=[smem, smem, ANY, vmem],
         out_specs=ANY,
         scratch_shapes=[
+            pltpu.VMEM(x_vals.shape, kind),
             pltpu.VMEM(rows, kind),
             pltpu.VMEM((count, wide), kind),
             pltpu.VMEM((octet, lanes), kind),
@@ -658,6 +671,7 @@
             dma((2 * row_devices, 4)),
             dma((supers, 4)),
             dma((4,)),
+            dma((count,)),
         ],
         compiler_params=pltpu.CompilerParams(
             collective_id=0, has_side_effects=True, vmem_limit_bytes=60 * 2**20
@@ -686,10 +700,9 @@
     late = (residue < spot).astype(jnp.int32)
     out_ref[...] = jnp.zeros_like(out_ref)
 
-    @pl.loop(0, rows)
-    def _(n):
+    for n in range(rows):
         origin = origins[lax.rem(first + n, count)]
-        at = pl.ds(pl.multiple_of(n * edge, edge), edge)
+        at = slice(n * edge, (n + 1) * edge)
         base = origin - 2 + late + count
         made = []
         for w in range(width // lanes):

time: 181 us -> 158 us (0.87); the launches traced: 181 us -> 156 us
  Pallas kernels: 181 us -> 156 us
    pallas_call x1, Pallas kernels: 168 us -> 145 us  [band_step(): pl.pallas_call(functools.partial(core_kernel, panels, scale), out_shape=j...]
    pallas_call x1, Pallas kernels: 12.8 us -> 10.6 us  [place_blocks(): pl.pallas_call(functools.partial(place_kernel, panels), out_shape=jax.Sha...]
where the time goes in v4:
time: 158 us; the launch traced here: 156 us
  Pallas kernels  156 us (99%)
    pallas_call x1, Pallas kernels, band_step(): pl.pallas_call(functools.partial(core_kernel, panels, scale), out_shape=j...  145 us
    pallas_call x1, Pallas kernels, place_blocks(): pl.pallas_call(functools.partial(place_kernel, panels), out_shape=jax.Sha...  10.6 us

profile of v4, /device:TPU:3, one launch (start us, length us, event | category | flops | bytes accessed | tf_op | source)
XLA Modules:
  0.0 155.7 jit_solution(9745709370221165624)
XLA Ops:
  0.0 145.2 %band_step.1.parts_ref = bf16[8,4,2,64,256]{4,3,2,1,0:T(8,128)(2,1)} custom-call(s32[8,32]{1,0:T(8,128)} %flags.1, s32[256]{0:T(256)} %perm.3, bf16[8,32,4096]{2,1,0:T(8,128)(2,1)} %x_vals.1, s32[8,32]{1,0:T(8,128)} %flags.1), custom_call_target="tpu_custom_call" | custom-call | tf_op jit(solution)/shard_map/band_step/pallas_call | solution.py:642
  145.2 10.6 %place_blocks.1 = bf16[4096,2048]{1,0:T(8,128)(2,1)} custom-call(s32[256]{0:T(256)} %perm.3, bf16[8,4,2,64,256]{4,3,2,1,0:T(8,128)(2,1)} %band_step.1.parts_ref), custom_call_target="tpu_custom_call" | custom-call | tf_op jit(solution)/shard_map/place_blocks/pallas_call | solution.py:727

commit v5 on v4

--- a/solution.py
+++ b/solution.py
@@ -536,11 +536,14 @@
 
     own_terms(tiles)
     second_halo = halo(square, square_sems)
-    turns = (1, 2, 0, 3)
-    waits = {1: (0,), 0: (1,), 2: (2,), 3: (3,)}
+    turns = (0, 3, 1, 2)
+    reads = {0: (0, 1), 1: (0,), 2: (2,), 3: (2, 3)}
+    waited = set()
     for t in turns:
-        for n in waits[t]:
-            first_halo[n].wait_recv()
+        for n in reads[t]:
+            if n not in waited:
+                first_halo[n].wait_recv()
+                waited.add(n)
         halo_terms(tiles, t)
         for r in range(count):
             at = slice(r * edge, (r + 1) * edge)
@@ -548,6 +551,7 @@
         second_halo[sends[t]].start()
 
     own_terms(square)
+    turns = (1, 2, 0, 3)
     def delivery(t, n):
         dest, h = n // pair, n % pair
         return remote(
@@ -574,9 +578,12 @@
             def _(n=n):
                 away(delivery(t, n))
 
+    waited = set()
     for t in turns:
-        for n in waits[t]:
-            second_halo[n].wait_recv()
+        for n in reads[t]:
+            if n not in waited:
+                second_halo[n].wait_recv()
+                waited.add(n)
         halo_terms(square, t)
         for r in range(count):
             at = slice(r * edge, (r + 1) * edge)
@@ -680,59 +687,110 @@
     )(occupancy, perm, x_vals, occupancy)
 
 
-def place_kernel(panels, perm, parts_ref, out_ref, origins):
-    supers, groups, halves, edge, width = parts_ref.shape
+def place_kernel(panels, perm, parts_in, out, parts, canvas, origins, load_sem, out_sems):
+    supers, groups, halves, edge, width = parts.shape
+    depth, tall = canvas.shape[:2]
+    chunk = tall // edge
     count = supers * groups
     lanes = 2 * edge
-    rows = out_ref.shape[0] // edge
+    steps = halves * count // chunk
     half = lax.broadcasted_iota(jnp.int32, (edge, lanes), 1) // edge
-    first = pl.program_id(0) * rows
-    e = first // count
-
-    @pl.when(first == 0)
-    def _():
-        @pl.loop(0, count)
-        def _(n):
-            origins[perm[n * panels] % count] = n
+    load = pltpu.make_async_copy(parts_in, parts, load_sem)
+    load.start()
+    for n in range(depth):
+        canvas[n] = jnp.zeros(canvas.shape[1:], canvas.dtype)
+
+    @pl.loop(0, count)
+    def _(n):
+        origins[perm[n * panels] % count] = n
 
     residue = residue_of(perm, panels, count, lax.axis_index("col"))
-    spot = residue_of(perm, panels, count, lax.axis_index("row") * halves + e)
-    late = (residue < spot).astype(jnp.int32)
-    out_ref[...] = jnp.zeros_like(out_ref)
-
-    for n in range(rows):
-        origin = origins[lax.rem(first + n, count)]
-        at = slice(n * edge, (n + 1) * edge)
-        base = origin - 2 + late + count
-        made = []
-        for w in range(width // lanes):
-            tile = parts_ref[
-                origin // groups, lax.rem(origin, groups), e, :, w * lanes : (w + 1) * lanes
-            ].astype(jnp.float32)
-            rolled = pltpu.roll(tile, edge, 1)
-            for side in range(2):
-                block = perm[lax.rem(base + 2 * w + side, count) * panels] % count
-                odd = lax.rem(block, 2)
-                value = jnp.where(odd == side, tile, rolled)
-                value = jnp.where(half == odd, value, 0.0).astype(out_ref.dtype)
-                made.append((pl.ds(pl.multiple_of((block // 2) * lanes, lanes), lanes), value))
-        for to, value in made:
-            out_ref[at, to] += value
+    first = lax.axis_index("row") * halves
+    late = [
+        (residue < residue_of(perm, panels, count, first + e)).astype(jnp.int32)
+        for e in range(halves)
+    ]
+    blank = jnp.zeros((edge, lanes), canvas.dtype)
+    load.wait()
+
+    def copy_of(step, slot):
+        to = pl.ds(pl.multiple_of(step * tall, tall), tall)
+        return pltpu.make_async_copy(canvas.at[slot], out.at[to], out_sems.at[slot])
+
+    def lanes_of(block):
+        return pl.ds(pl.multiple_of((block // 2) * lanes, lanes), lanes)
+
+    def blocks_of(step, n):
+        e = step * chunk // count
+        origin = origins[lax.rem(step * chunk + n, count)]
+        shift = late[0]
+        for k in range(1, halves):
+            shift = jnp.where(e == k, late[k], shift)
+        base = origin - 2 + shift + count
+        return e, origin, [
+            perm[lax.rem(base + o, count) * panels] % count for o in range(width // edge)
+        ]
+
+    def fill(step, slot):
+        for n in range(chunk):
+            e, origin, blocks = blocks_of(step, n)
+            at = slice(n * edge, (n + 1) * edge)
+            made = []
+            for w in range(width // lanes):
+                tile = parts[
+                    origin // groups, lax.rem(origin, groups), e, :, w * lanes : (w + 1) * lanes
+                ].astype(jnp.float32)
+                rolled = pltpu.roll(tile, edge, 1)
+                for side in range(2):
+                    odd = lax.rem(blocks[2 * w + side], 2)
+                    value = jnp.where(odd == side, tile, rolled)
+                    value = jnp.where(half == odd, value, 0.0).astype(canvas.dtype)
+                    made.append((lanes_of(blocks[2 * w + side]), value))
+            for to, value in made:
+                canvas[slot, at, to] += value
+
+    def clear(step, slot):
+        for n in range(chunk):
+            for block in blocks_of(step, n)[2]:
+                canvas[slot, n * edge : (n + 1) * edge, lanes_of(block)] = blank
+
+    @pl.loop(0, steps // depth)
+    def _(r):
+        for slot in range(depth):
+            step = r * depth + slot
+
+            @pl.when(r > 0)
+            def _(step=step, slot=slot):
+                copy_of(step - depth, slot).wait()
+                clear(step - depth, slot)
+
+            fill(step, slot)
+            copy_of(step, slot).start()
+
+    for slot in range(depth):
+        copy_of(steps - depth + slot, slot).wait()
 
 
 def place_blocks(parts, perm, panels):
     supers, groups, halves, edge, width = parts.shape
     count = supers * groups
-    rows = min(count, 8)
+    chunk, depth = 8, 4
+    dma = pltpu.SemaphoreType.DMA
     return pl.pallas_call(
         functools.partial(place_kernel, panels),
         out_shape=jax.ShapeDtypeStruct((halves * count * edge, count * edge), parts.dtype),
         grid_spec=pltpu.PrefetchScalarGridSpec(
             num_scalar_prefetch=1,
-            grid=(halves * count // rows,),
-            in_specs=[pl.BlockSpec(parts.shape, lambda g, *_: (0, 0, 0, 0, 0))],
-            out_specs=pl.BlockSpec((rows * edge, count * edge), lambda g, *_: (g, 0)),
-            scratch_shapes=[pltpu.SMEM((count,), jnp.int32)],
+            grid=(1,),
+            in_specs=[ANY],
+            out_specs=ANY,
+            scratch_shapes=[
+                pltpu.VMEM(parts.shape, parts.dtype),
+                pltpu.VMEM((depth, chunk * edge, count * edge), parts.dtype),
+                pltpu.SMEM((count,), jnp.int32),
+                dma,
+                dma((depth,)),
+            ],
         ),
         compiler_params=pltpu.CompilerParams(dimension_semantics=("arbitrary",)),
         name="place_blocks",

time: 158 us -> 154 us (0.975)
  Pallas kernels: 156 us -> 153 us
    pallas_call x1, Pallas kernels: 10.6 us -> 8.85 us  [place_blocks(): pl.pallas_call(functools.partial(place_kernel, panels), out_shape=jax.Sha...]
where the time goes in v5:
time: 154 us; the launch traced here: 153 us
  Pallas kernels  153 us (99%)
    pallas_call x1, Pallas kernels, band_step(): pl.pallas_call(functools.partial(core_kernel, panels, scale), out_shape=j...  144 us
    pallas_call x1, Pallas kernels, place_blocks(): pl.pallas_call(functools.partial(place_kernel, panels), out_shape=jax.Sha...  8.85 us

profile of v5, /device:TPU:3, one launch (start us, length us, event | category | flops | bytes accessed | tf_op | source)
XLA Modules:
  0.0 153.2 jit_solution(5163375837390775393)
XLA Ops:
  0.0 144.1 %band_step.1.parts_in = bf16[8,4,2,64,256]{4,3,2,1,0:T(8,128)(2,1)} custom-call(s32[8,32]{1,0:T(8,128)} %flags.1, s32[256]{0:T(256)} %perm.3, bf16[8,32,4096]{2,1,0:T(8,128)(2,1)} %x_vals.1, s32[8,32]{1,0:T(8,128)} %flags.1), custom_call_target="tpu_custom_call" | custom-call | tf_op jit(solution)/shard_map/band_step/pallas_call | solution.py:649
  144.2 8.8 %place_blocks.1 = bf16[4096,2048]{1,0:T(8,128)(2,1)} custom-call(s32[256]{0:T(256)} %perm.3, bf16[8,4,2,64,256]{4,3,2,1,0:T(8,128)(2,1)} %band_step.1.parts_in), custom_call_target="tpu_custom_call" | custom-call | tf_op jit(solution)/shard_map/place_blocks/pallas_call | solution.py:779

commit v6 on v5

--- a/solution.py
+++ b/solution.py
@@ -393,6 +393,8 @@
         )
         late[n : n + 1, :] = (own < spot).astype(jnp.float32)
 
+    load_of(0).wait()
+    relay_row(0)
     expected = 5 + len(receivers)
     pl.semaphore_wait(barrier, jnp.where(owner == place.core, expected - 1, expected))
 
@@ -400,7 +402,7 @@
 
     @pl.loop(0, count + 1)
     def _(t):
-        @pl.when(t < count)
+        @pl.when(jnp.logical_and(t > 0, t < count))
         def _():
             load_of(t).wait()
             relay_row(t)
@@ -551,7 +553,7 @@
         second_halo[sends[t]].start()
 
     own_terms(square)
-    turns = (1, 2, 0, 3)
+    turns = (2, 1, 3, 0)
     def delivery(t, n):
         dest, h = n // pair, n % pair
         return remote(
@@ -774,7 +776,7 @@
 def place_blocks(parts, perm, panels):
     supers, groups, halves, edge, width = parts.shape
     count = supers * groups
-    chunk, depth = 8, 4
+    chunk, depth = 4, 16
     dma = pltpu.SemaphoreType.DMA
     return pl.pallas_call(
         functools.partial(place_kernel, panels),

time: 154 us -> 153 us (level)
  no operation moved by 1% of the time
where the time goes in v6:
time: 153 us
  Pallas kernels  153 us (100%)
    pallas_call x1, Pallas kernels, band_step(): pl.pallas_call(functools.partial(core_kernel, panels, scale), out_shape=j...  144 us
    pallas_call x1, Pallas kernels, place_blocks(): pl.pallas_call(functools.partial(place_kernel, panels), out_shape=jax.Sha...  8.5 us

profile of v6, /device:TPU:3, one launch (start us, length us, event | category | flops | bytes accessed | tf_op | source)
XLA Modules:
  0.0 152.9 jit_solution(7806262440499734971)
XLA Ops:
  0.0 144.2 %band_step.1.parts_in = bf16[8,4,2,64,256]{4,3,2,1,0:T(8,128)(2,1)} custom-call(s32[8,32]{1,0:T(8,128)} %flags.1, s32[256]{0:T(256)} %perm.3, bf16[8,32,4096]{2,1,0:T(8,128)(2,1)} %x_vals.1, s32[8,32]{1,0:T(8,128)} %flags.1), custom_call_target="tpu_custom_call" | custom-call | tf_op jit(solution)/shard_map/band_step/pallas_call | solution.py:651
  144.2 8.5 %place_blocks.1 = bf16[4096,2048]{1,0:T(8,128)(2,1)} custom-call(s32[256]{0:T(256)} %perm.3, bf16[8,4,2,64,256]{4,3,2,1,0:T(8,128)(2,1)} %band_step.1.parts_in), custom_call_target="tpu_custom_call" | custom-call | tf_op jit(solution)/shard_map/place_blocks/pallas_call | solution.py:781
